TPU v7x, 32 devices: a whole 2x2x4 slice. The times are simulated.
32 devices in a mesh: tm: 16 (over z, y, core), series: 2 (over x).
Axes of the slice: x: 2, y: 2, z: 4, core: 2. Of those that a mesh axis runs over, the one named last changes fastest.
Arguments:
- history: bfloat16 [4, 4096, 1024], P('series', 'tm'), may hold values from -36 to 36
- lengths: int32 [4], P('series'), may hold values from 512 to 4096
- head_window: int32 [16], replicated, may hold values from 32 to 512, as said below
- input_proj: bfloat16 [1024, 3072], replicated
- output_proj: bfloat16 [1024, 1024], replicated, may hold values from -0.1875 to 0.1875
- mixer_down: bfloat16 [1024, 512], replicated, may hold values from -0.1875 to 0.1875
- mixer_up: bfloat16 [512, 1024], replicated, may hold values from -0.25 to 0.25
- series_mix: bfloat16 [4, 4], replicated, may hold values from -3 to 3
Outputs:
- layer_out: bfloat16 [4, 4096, 1024], P('series', 'tm')
Inputs may be any that keep to these rules, and one draw needn't show every extreme that they name: `head_window`: some head has exactly 512.
All inputs are finite; a program needn't handle non-finite values.
Results may differ from a plain program's by a relative error of at most 0.0065.
Values may be sent and summed in bfloat16 or wider, within the bound.
No kernel may reach another device: no remote copies, remote signals or barrier semaphores. Data moves between devices by JAX's collectives and lax.ppermute only.
A program may use at most 128 MiB of HBM per device.

v0:
```python
import jax
import jax.numpy as jnp
from jax import lax
from jax.sharding import PartitionSpec as P

HEADS = 16
WINDOW = 512


def from_behind(block, axis, distance):
    devices = range(lax.axis_size(axis))
    route = [(i - distance, i) for i in devices if i - distance in devices]
    return lax.ppermute(block, axis, route)


def attend_series(queries, keys_values, length, head_window, query_first, key_first, patches):
    query_rows = queries.shape[0]
    model_width = queries.shape[1]
    key_rows = keys_values.shape[0]
    head_size = model_width // HEADS
    group_heads = min(4, HEADS)
    group_count = HEADS // group_heads
    group_width = group_heads * head_size
    query_pos = query_first + jnp.arange(query_rows, dtype=jnp.int32)
    key_pos = key_first + jnp.arange(key_rows, dtype=jnp.int32)
    key_valid = (key_pos >= patches - length) & (key_pos < patches)
    distance = jnp.abs(query_pos[:, None] - key_pos[None, :])

    def per_group(group_index):
        column = group_index * group_width
        group_queries = lax.dynamic_slice_in_dim(queries, column, group_width, 1).reshape(
            query_rows, group_heads, head_size
        )
        group_keys = lax.dynamic_slice_in_dim(keys_values, column, group_width, 1).reshape(
            key_rows, group_heads, head_size
        )
        group_values = lax.dynamic_slice_in_dim(
            keys_values, model_width + column, group_width, 1
        ).reshape(key_rows, group_heads, head_size)
        reaches = lax.dynamic_slice_in_dim(head_window, group_index * group_heads, group_heads, 0)
        scores = jnp.einsum(
            "qhd,khd->hqk", group_queries, group_keys, preferred_element_type=jnp.float32
        ) * head_size ** (-0.5)
        allowed = (distance[None, :, :] <= reaches[:, None, None]) & key_valid[None, None, :]
        scores = jnp.where(allowed, scores, -1e30)
        largest = jnp.max(scores, axis=-1, keepdims=True)
        weights = jnp.exp(scores - largest)
        totals = jnp.sum(weights, axis=-1)
        probabilities = weights.astype(jnp.bfloat16)
        combined = (
            jnp.einsum(
                "hqk,khd->qhd", probabilities, group_values, preferred_element_type=jnp.float32
            )
            / jnp.transpose(totals)[:, :, None]
        )
        return combined.reshape(query_rows, group_width)

    grouped = lax.map(per_group, jnp.arange(group_count, dtype=jnp.int32))
    combined = jnp.transpose(grouped, (1, 0, 2)).reshape(query_rows, model_width)
    query_valid = query_pos >= patches - length
    return jnp.where(query_valid[:, None], combined, 0.0).astype(jnp.bfloat16)


def on_device(
    history, lengths, head_window, input_proj, output_proj, mixer_down, mixer_up, series_mix
):
    local_series, local_patches, model_width = history.shape
    packed = jnp.einsum(
        "spd,de->spe", history, input_proj, preferred_element_type=jnp.float32
    ).astype(jnp.bfloat16)
    queries = packed[:, :, :model_width]
    keys_values = packed[:, :, model_width:]
    hops_count = -(-WINDOW // local_patches)
    earlier = []
    following = []
    kv_weight = input_proj[:, model_width:]
    for offset in range(1, hops_count + 1):
        before_rows = from_behind(history, "tm", offset)
        after_rows = from_behind(history, "tm", -offset)
        earlier.insert(
            0,
            jnp.einsum(
                "spd,de->spe", before_rows, kv_weight, preferred_element_type=jnp.float32
            ).astype(jnp.bfloat16),
        )
        following.append(
            jnp.einsum(
                "spd,de->spe", after_rows, kv_weight, preferred_element_type=jnp.float32
            ).astype(jnp.bfloat16)
        )
    context = jnp.concatenate(earlier + [keys_values] + following, axis=1)
    position = lax.axis_index("tm")
    patches = local_patches * lax.axis_size("tm")
    query_first = position * local_patches
    key_first = (position - hops_count) * local_patches

    def per_series(inputs):
        series_queries, series_context, length = inputs
        return attend_series(
            series_queries, series_context, length, head_window, query_first, key_first, patches
        )

    attended = lax.map(per_series, (queries, context, lengths))
    hidden = (
        history.astype(jnp.float32)
        + jnp.einsum("spd,de->spe", attended, output_proj, preferred_element_type=jnp.float32)
    ).astype(jnp.bfloat16)
    branch = jnp.einsum(
        "spd,dc->spc", hidden, mixer_down, preferred_element_type=jnp.float32
    ).astype(jnp.bfloat16)
    series_first = lax.axis_index("series") * local_series
    own_rows = lax.dynamic_slice_in_dim(series_mix, series_first, local_series, 0)
    combined = jnp.einsum(
        "ab,bpc->apc",
        own_rows,
        lax.all_gather(branch, "series", axis=0, tiled=True),
        preferred_element_type=jnp.float32,
    )
    combined = combined.astype(jnp.bfloat16)
    update = jnp.einsum("spc,cd->spd", combined, mixer_up, preferred_element_type=jnp.float32)
    return (hidden.astype(jnp.float32) + update).astype(jnp.bfloat16)


def solution(mesh):
    in_specs = (P("series", "tm", None), P("series"), P(), P(), P(), P(), P(), P())
    out_specs = P("series", "tm", None)
    return jax.shard_map(
        on_device, mesh=mesh, in_specs=in_specs, out_specs=out_specs, check_vma=False
    )
```

profile of v0, /device:TPU:0, one launch (start us, length us, event | category | flops | bytes accessed | tf_op | source)
XLA Modules:
  0.0 253.0 jit_solution(13896051567737535328)
XLA Ops:
  6.5 6.0 %collective-permute-start = (bf16[2,256,1024]{2,1,0:T(8,128)(2,1)}, bf16[2,256,1024]{2,1,0:T(8,128)(2,1)}, u32[]{:S(2)}, u32[]{:S(2)}) collective-permute-start(bf16[2,256,1024]{2,1,0:T(8,128)(2,1)} %param.12), channel_id=1, source_target_pairs={{0,4},{2,6},{4,8},{6,10},{8,12},{10,14},{12,16},{14,18},{16,20},{1... | collective-permute-start | bytes 3145736 | tf_op jit(solution)/shard_map/ppermute | solution.py:13
  12.5 2.5 collective-permute-start.1
  17.6 6.5 %fusion.22 = bf16[2,256,3072]{2,1,0:T(8,128)(2,1)S(1)} fusion(bf16[2,256,1024]{2,1,0:T(8,128)(2,1)} %param.12, bf16[1024,3072]{1,0:T(8,128)(2,1)} %param.15), kind=kOutput, calls=%fused_computation.29 | convolution fusion | flops 3222798336 | bytes 10485760 | tf_op jit(solution)/shard_map/spd,de->spe/dot_general | solution.py:68
  24.2 1.6 copy-done.2
  26.9 42.2 %collective-permute-done = bf16[2,256,1024]{2,1,0:T(8,128)(2,1)} collective-permute-done((bf16[2,256,1024]{2,1,0:T(8,128)(2,1)}, bf16[2,256,1024]{2,1,0:T(8,128)(2,1)}, u32[]{:S(2)}, u32[]{:S(2)}) %collective-permute-start) | collective-permute-done | bytes 1048608 | tf_op jit(solution)/shard_map/ppermute | solution.py:13
  69.1 5.0 %fusion.36 = bf16[2,1280,2048]{2,1,0:T(8,128)(2,1)S(1)} fusion(bf16[2,256,1024]{2,1,0:T(8,128)(2,1)} %collective-permute-done, bf16[1024,3072]{1,0:T(8,128)(2,1)} %param.15), kind=kOutput, calls=%fused_computation.39 | convolution fusion | flops 2148532224 | bytes 7340032 | tf_op jit(solution)/shard_map/spd,de->spe/dot_general | solution.py:82
  74.2 5.0 %fusion.42 = bf16[2,1280,2048]{2,1,0:T(8,128)(2,1)S(1)} fusion(bf16[2,1280,2048]{2,1,0:T(8,128)(2,1)S(1)} %fusion.36, bf16[2,256,1024]{2,1,0:T(8,128)(2,1)} %collective-permute-done.1, bf16[1024,3072]{1,0:T(8,128)(2,1)} %param.15), kind=kOutput, calls=%fused_computation.41 | convolution fusion | flops 2148532224 | bytes 7340032 | tf_op jit(solution)/shard_map/spd,de->spe/dot_general | solution.py:82
  79.4 3.6 %fusion.48 = bf16[2,1280,2048]{2,1,0:T(8,128)(2,1)S(1)} fusion(bf16[2,1280,2048]{2,1,0:T(8,128)(2,1)S(1)} %slice_dynamic-update-slice_fusion, bf16[2,256,1024]{2,1,0:T(8,128)(2,1)} %collective-permute-done.2, bf16[1024,3072]{1,0:T(8,128)(2,1)S(1)} %bitcast.116), kind=kOutput, calls=%fused_computation.43 | convolution fusion | flops 2148532224 | bytes 7340032 | tf_op jit(solution)/shard_map/spd,de->spe/dot_general | solution.py:87
  83.0 2.3 fusion.54
  85.3 4.0 %copy-done.1 = bf16[2,1280,2048]{2,1,0:T(8,128)(2,1)} copy-done((bf16[2,1280,2048]{2,1,0:T(8,128)(2,1)}, bf16[2,1280,2048]{2,1,0:T(8,128)(2,1)S(1)}, u32[]{:S(2)}) %copy-start.1) | copy-done | bytes 10485784
  89.3 118.7 %while.33 = (s32[]{:T(128)}, bf16[2,256,1024]{1,2,0:T(8,128)(2,1)}, s32[]{:T(128)}, s32[2]{0:T(128)S(1)}, bf16[2,256,1024]{2,1,0:T(8,128)(2,1)}, /*index=5*/bf16...) while((s32[]{:T(128)}, bf16[2,256,1024]{1,2,0:T(8,128)(2,1)}, ...), condition=%wide.region_5.6_spmd, body=%wide.region_0.5_spmd.sunk | while | flops 348394496 | bytes 47223572 | solution.py:103
  90.6 5.6 %constant_dynamic-slice_fusion.9 = bf16[1,1280,2048]{2,1,0:T(8,128)(2,1)} fusion(bf16[2,1280,2048]{2,1,0:T(8,128)(2,1)} %get-tuple-element.545, s32[]{:T(128)} %get-tuple-element.521), kind=kLoop, calls=%fused_computation.25.clone.1 | loop fusion | bytes 10485764 | tf_op jit(solution)/shard_map/while/body/jit(dynamic_index_in_dim)/dynamic_slice | solution.py:103
  96.2 7.9 %copy.26 = bf16[1,1280,2048]{1,2,0:T(8,128)(2,1)} copy(bf16[1,1280,2048]{2,1,0:T(8,128)(2,1)} %constant_dynamic-slice_fusion.9) | data formatting | bytes 10485760 | tf_op jit(solution)/shard_map/while/body/jit(dynamic_index_in_dim)/dynamic_slice | solution.py:103
  106.7 40.1 %while.34 = (s32[]{:T(128)}, bf16[4,256,256]{1,2,0:T(8,128)(2,1)}, s32[4]{0:T(128)}, bf16[1280,2048]{0,1:T(8,128)(2,1)}, s32[16]{0:T(128)}, /*index=5*/bf16[256,...) while((s32[]{:T(128)}, bf16[4,256,256]{1,2,0:T(8,128)(2,1)}, ...), condition=%wide.region_4.4_spmd.clone, body=%wide.region_1.3_spmd.clone.sunk | while | flops 348130304 | bytes 23098768 | solution.py:58
  112.3 1.8 fusion.98
  122.3 1.8 fusion.98
  132.3 1.8 fusion.98
  142.3 1.8 fusion.98
  146.7 1.9 fusion.92
  149.9 5.6 %constant_dynamic-slice_fusion.9 = bf16[1,1280,2048]{2,1,0:T(8,128)(2,1)} fusion(bf16[2,1280,2048]{2,1,0:T(8,128)(2,1)} %get-tuple-element.545, s32[]{:T(128)} %get-tuple-element.521), kind=kLoop, calls=%fused_computation.25.clone.1 | loop fusion | bytes 10485764 | tf_op jit(solution)/shard_map/while/body/jit(dynamic_index_in_dim)/dynamic_slice | solution.py:103
  155.5 7.9 %copy.26 = bf16[1,1280,2048]{1,2,0:T(8,128)(2,1)} copy(bf16[1,1280,2048]{2,1,0:T(8,128)(2,1)} %constant_dynamic-slice_fusion.9) | data formatting | bytes 10485760 | tf_op jit(solution)/shard_map/while/body/jit(dynamic_index_in_dim)/dynamic_slice | solution.py:103
  166.0 40.1 %while.34 = (s32[]{:T(128)}, bf16[4,256,256]{1,2,0:T(8,128)(2,1)}, s32[4]{0:T(128)}, bf16[1280,2048]{0,1:T(8,128)(2,1)}, s32[16]{0:T(128)}, /*index=5*/bf16[256,...) while((s32[]{:T(128)}, bf16[4,256,256]{1,2,0:T(8,128)(2,1)}, ...), condition=%wide.region_4.4_spmd.clone, body=%wide.region_1.3_spmd.clone.sunk | while | flops 348130304 | bytes 23098768 | solution.py:58
  171.6 1.8 fusion.98
  181.6 1.8 fusion.98
  191.6 1.8 fusion.98
  201.7 1.8 fusion.98
  206.1 1.9 fusion.92
  208.0 3.0 %add_convert_fusion.1 = bf16[2,256,1024]{2,1,0:T(8,128)(2,1)S(1)} fusion(bf16[2,256,1024]{2,1,0:T(8,128)(2,1)} %param.12, bf16[2,256,1024]{1,2,0:T(8,128)(2,1)} %get-tuple-element.223, bf16[1024,1024]{1,0:T(8,128)(2,1)S(1)} %copy-done), kind=kOutput, calls=%fused_computation.54 | convolution fusion | flops 1075314688 | bytes 5242880 | tf_op jit(solution)/shard_map/spd,de->spe/dot_general | solution.py:106
  211.9 1.5 convolution_convert_fusion
  213.5 27.6 %all-gather.2.cloned.1.call-done = bf16[4,256,512]{2,1,0:T(8,128)(2,1)} async-done(((bf16[2,256,512]{2,1,0:T(8,128)(2,1)}), bf16[4,256,512]{2,1,0:T(8,128)(2,1)}) %all-gather.2.cloned.1.call-update) | async-done | bytes 1048592 | tf_op jit(solution)/shard_map/all_gather | solution.py:116
  241.1 2.1 fusion.67
  243.2 2.9 %add_convert_fusion = bf16[2,256,1024]{2,1,0:T(8,128)(2,1)} fusion(bf16[2,256,1024]{2,1,0:T(8,128)(2,1)} %copy-done.8, bf16[512,1024]{1,0:T(8,128)(2,1)S(1)} %copy-done.5, bf16[2,256,512]{2,0,1:T(2,128)(2,1)S(1)} %fusion.67), kind=kOutput, calls=%fused_computation.53 | convolution fusion | flops 538443776 | bytes 3670016 | tf_op jit(solution)/shard_map/spc,cd->spd/dot_general | solution.py:120
  (119 shorter events, 67.8 us)
Async XLA Ops:
  6.5 201.5 %copy-start = (bf16[1024,1024]{1,0:T(8,128)(2,1)S(1)}, bf16[1024,1024]{1,0:T(8,128)(2,1)}, u32[]{:S(2)}) copy-start(bf16[1024,1024]{1,0:T(8,128)(2,1)} %param.16) | copy-start | bytes 6291460
  6.5 234.5 %all-gather.2.cloned.1.call-start = ((), (), s32[]{:S(2)}) async-start(), calls=%async_computation | async-start | bytes 1572864 | tf_op jit(solution)/shard_map/all_gather | solution.py:116
  6.5 62.6 %collective-permute-start = (bf16[2,256,1024]{2,1,0:T(8,128)(2,1)}, bf16[2,256,1024]{2,1,0:T(8,128)(2,1)}, u32[]{:S(2)}, u32[]{:S(2)}) collective-permute-start(bf16[2,256,1024]{2,1,0:T(8,128)(2,1)} %param.12), channel_id=1, source_target_pairs={{0,4},{2,6},{4,8},{6,10},{8,12},{10,14},{12,16},{14,18},{16,20},{1... | collective-permute-start | bytes 3145736 | tf_op jit(solution)/shard_map/ppermute | solution.py:13
  12.5 61.6 %collective-permute-start.1 = (bf16[2,256,1024]{2,1,0:T(8,128)(2,1)}, bf16[2,256,1024]{2,1,0:T(8,128)(2,1)}, u32[]{:S(2)}, u32[]{:S(2)}) collective-permute-start(bf16[2,256,1024]{2,1,0:T(8,128)(2,1)} %param.12), channel_id=1, source_target_pairs={{0,2},{2,4},{4,6},{6,8},{8,10},{10,12},{12,14},{14,16},{16,18},{18... | collective-permute-start | bytes 3145736 | tf_op jit(solution)/shard_map/ppermute | solution.py:13
  15.0 64.3 %collective-permute-start.2 = (bf16[2,256,1024]{2,1,0:T(8,128)(2,1)}, bf16[2,256,1024]{2,1,0:T(8,128)(2,1)}, u32[]{:S(2)}, u32[]{:S(2)}) collective-permute-start(bf16[2,256,1024]{2,1,0:T(8,128)(2,1)} %param.12), channel_id=1, source_target_pairs={{2,0},{4,2},{6,4},{8,6},{10,8},{12,10},{14,12},{16,14},{18,16},{20... | collective-permute-start | bytes 3145736 | tf_op jit(solution)/shard_map/ppermute | solution.py:13
  16.3 66.7 %collective-permute-start.3 = (bf16[2,256,1024]{2,1,0:T(8,128)(2,1)}, bf16[2,256,1024]{2,1,0:T(8,128)(2,1)S(1)}, u32[]{:S(2)}, u32[]{:S(2)}) collective-permute-start(bf16[2,256,1024]{2,1,0:T(8,128)(2,1)} %param.12), channel_id=1, source_target_pairs={{4,0},{6,2},{8,4},{10,6},{12,8},{14,10},{16,12},{18,14},{20,16},{2... | collective-permute-start | bytes 3145736 | tf_op jit(solution)/shard_map/ppermute | solution.py:13
  24.2 1.6 copy-start.2
  69.1 10.2 %slice-start = ((s8[6291456]{0:T(1024)(128)(4,1)}), s8[4194304]{0:T(1024)(128)(4,1)S(1)}, s32[]{:S(2)}) async-start(s8[6291456]{0:T(1024)(128)(4,1)} %bitcast.115), calls=%async_computation.1 | async-start | bytes 8388608
  74.1 5.0 %copy-start.3 = (bf16[2,256,3072]{2,1,0:T(8,128)(2,1)S(1)}, bf16[2,256,3072]{2,1,0:T(8,128)(2,1)}, u32[]{:S(2)}) copy-start(bf16[2,256,3072]{2,1,0:T(8,128)(2,1)} %copy-done.2) | copy-start | bytes 9437188
  74.1 5.2 %slice-start.1 = ((s8[6291456]{0:T(1024)(128)(4,1)}), s8[2097152]{0:T(1024)(128)(4,1)S(1)}, s32[]{:S(2)}) async-start(s8[6291456]{0:T(1024)(128)(4,1)} %bitcast.115), calls=%async_computation.2 | async-start | bytes 4194304
  83.0 6.4 %copy-start.7 = (s32[2]{0:T(128)S(1)}, s32[2]{0:T(128)}, u32[]{:S(2)}) copy-start(s32[2]{0:T(128)} %param.13) | copy-start | bytes 28
  85.3 4.0 %copy-start.1 = (bf16[2,1280,2048]{2,1,0:T(8,128)(2,1)}, bf16[2,1280,2048]{2,1,0:T(8,128)(2,1)S(1)}, u32[]{:S(2)}) copy-start(bf16[2,1280,2048]{2,1,0:T(8,128)(2,1)S(1)} %fusion.54) | copy-start | bytes 31457284
  208.0 4.0 %copy-start.4 = (bf16[1024,512]{1,0:T(8,128)(2,1)S(1)}, bf16[1024,512]{1,0:T(8,128)(2,1)}, u32[]{:S(2)}) copy-start(bf16[1024,512]{1,0:T(8,128)(2,1)} %param.17) | copy-start | bytes 3145732
  208.0 33.1 %copy-start.6 = (bf16[4,4]{1,0:T(4,128)(2,1)S(1)}, bf16[4,4]{1,0:T(4,128)(2,1)}, u32[]{:S(2)}) copy-start(bf16[4,4]{1,0:T(4,128)(2,1)} %param.19) | copy-start | bytes 100
  208.0 35.2 %copy-start.5 = (bf16[512,1024]{1,0:T(8,128)(2,1)S(1)}, bf16[512,1024]{1,0:T(8,128)(2,1)}, u32[]{:S(2)}) copy-start(bf16[512,1024]{1,0:T(8,128)(2,1)} %param.18) | copy-start | bytes 3145732
  211.0 1.0 copy-start.8
Sparse Core Ops, SparseCore 0:
  213.6 27.3 all-gather.1
where the time goes:
time: 255 us; the launch traced here: 253 us
  local copies, waits for them, and re-layouts  80 us (31%)
  waiting for transfers between devices  69.8 us (27%)
  matrix products  54.1 us (21%)
  other arithmetic  13.6 us (5%)
  between operations  13.6 us (5%)
  starting transfers between devices  11.1 us (4%)
  loops' own time  10.8 us (4%)
    ppermute x4, waiting for transfers between devices, from_behind(): return lax.ppermute(block, axis, route)  42.3 us
    dynamic_slice x10, local copies, waits for them, and re-layouts, on_device(): attended = lax.map(per_series, (queries, context, lengths))  32.4 us
    all_gather x1, waiting for transfers between devices, on_device(): lax.all_gather(branch, 'series', axis=0, tiled=True)  27.6 us
    dot_general x8, matrix products, per_group(): jnp.einsum('qhd,khd->hqk', group_queries, group_keys, preferred_element_t...  14.1 us
    ppermute x4, starting transfers between devices, from_behind(): return lax.ppermute(block, axis, route)  11.1 us
    dynamic_slice x8, local copies, waits for them, and re-layouts, per_group(): lax.dynamic_slice_in_dim(keys_values, column, group_width, 1)  11 us
    dot_general x2, matrix products, on_device(): jnp.einsum('spd,de->spe', before_rows, kv_weight, preferred_element_type=...  9.98 us
    another operation x2, loops' own time, attend_series(): grouped = lax.map(per_group, jnp.arange(group_count, dtype=jnp.int32))  9.47 us
  transfers between devices with their start and end apart: 5, of which 2 were waited for; matrix products, arithmetic and copies ran while one was open for 8% of the time, Pallas kernels for 0%

commit v1 on v0

v1 whole, which is shorter than its diff:
```python
import math

import jax
import jax.numpy as jnp
from jax import lax
from jax.experimental import pallas as pl
from jax.experimental.pallas import tpu as pltpu
from jax.sharding import PartitionSpec as P

HEADS = 16
WINDOW = 512
LANES = 128
MASKED = -1e30


def routes(count):
    place = lambda quad, chip, core: 4 * quad + 2 * chip + core
    last = count // 4 - 1
    chip_swap = [(i, i ^ 2) for i in range(count)]
    core_swap = [(i, i ^ 1) for i in range(count)]
    near, far = [], []
    for i in range(count):
        quad, chip, core = i // 4, (i // 2) % 2, i % 2
        down = quad - 1 if quad > 0 else None
        up = quad + 1 if quad < last else None
        near_quad, far_quad = (down, up) if chip == 0 else (up, down)
        if near_quad is not None:
            near.append((i, place(near_quad, chip, core)))
        if far_quad is not None:
            far.append((i, place(far_quad, chip, core)))
    return chip_swap, core_swap, near, far


def project(pieces, slots, weight, first_column, slot_count, buffer=None):
    rows, width = pieces[0].shape
    columns = weight.shape[1] - first_column
    chunk = min(512, columns)
    count = len(pieces)

    def body(slots_ref, *refs):
        piece_refs = refs[:count]
        weight_ref = refs[count]
        out_ref = refs[-1]
        for index in range(count):

            @pl.when(pl.program_id(1) == index)
            def _():
                out_ref[0] = jnp.dot(
                    piece_refs[index][...], weight_ref[...], preferred_element_type=jnp.float32
                ).astype(out_ref.dtype)

    in_specs = [pl.BlockSpec((rows, width), lambda j, i, s: (0, 0)) for _ in pieces]
    in_specs.append(
        pl.BlockSpec((width, chunk), lambda j, i, s: (0, first_column // chunk + j))
    )
    operands = list(pieces) + [weight]
    aliases = {}
    if buffer is not None:
        in_specs.append(pl.BlockSpec(memory_space=pl.ANY))
        operands.append(buffer)
        aliases = {len(operands): 0}
    flops = 2 * count * rows * width * columns
    return pl.pallas_call(
        body,
        out_shape=jax.ShapeDtypeStruct((slot_count, rows, columns), jnp.bfloat16),
        grid_spec=pltpu.PrefetchScalarGridSpec(
            num_scalar_prefetch=1,
            grid=(columns // chunk, count),
            in_specs=in_specs,
            out_specs=pl.BlockSpec((1, rows, chunk), lambda j, i, s: (s[i], 0, j)),
        ),
        input_output_aliases=aliases,
        cost_estimate=pl.CostEstimate(
            flops=flops, bytes_accessed=2 * width * columns, transcendentals=0
        ),
        name="project",
    )(slots, *operands)


def attend(info, head_window, queries, buffer):
    rows, width = queries.shape
    head_size = width // HEADS
    pair_count = width // LANES
    reach = WINDOW // rows
    steps = 2 * reach + 1
    value_first = width // LANES
    cols = 2 * rows

    def body(info_ref, window_ref, query_ref, *refs):
        key_refs = refs[:steps]
        value_refs = refs[steps : 2 * steps]
        out_ref = refs[2 * steps]
        score_ref = refs[2 * steps + 1]
        pair = pl.program_id(0)
        query_first = info_ref[1]
        valid_first = info_ref[2]
        patches = info_ref[3]
        query = query_ref[...]
        lane = lax.broadcasted_iota(jnp.int32, query.shape, 1)
        zero = jnp.zeros_like(query)
        both = jnp.concatenate(
            [jnp.where(lane < head_size, query, zero), jnp.where(lane < head_size, zero, query)], 0
        )
        column = lax.broadcasted_iota(jnp.int32, (1, cols), 1)
        second = column >= rows
        window = jnp.where(second, window_ref[2 * pair + 1], window_ref[2 * pair])
        local = jnp.where(second, column - rows, column)
        lowest = jnp.maximum(local - window, valid_first - query_first)
        highest = jnp.minimum(local + window, patches - 1 - query_first)
        key_row = lax.broadcasted_iota(jnp.int32, (rows, cols), 0)
        largest = None
        for step in range(steps):
            first = (step - reach) * rows
            scores = lax.dot_general(
                key_refs[step][0],
                both,
                (((1,), (1,)), ((), ())),
                preferred_element_type=jnp.float32,
            )
            allowed = None
            if step <= reach:
                allowed = key_row >= lowest - first
            if step >= reach:
                upper = key_row <= highest - first
                allowed = upper if allowed is None else allowed & upper
            scores = jnp.where(allowed, scores, MASKED)
            score_ref[step] = scores
            top = jnp.max(scores, axis=0, keepdims=True)
            largest = top if largest is None else jnp.maximum(largest, top)
        ones = jnp.ones((16, rows), jnp.bfloat16)
        sums = [None, None]
        for step in range(steps):
            weights = jnp.exp2(score_ref[step] - largest).astype(jnp.bfloat16)
            values = value_refs[step][0].T
            for half in range(2):
                left = jnp.concatenate(
                    [values[half * head_size : (half + 1) * head_size], ones], 0
                )
                part = jnp.dot(
                    left,
                    weights[:, half * rows : (half + 1) * rows],
                    preferred_element_type=jnp.float32,
                )
                sums[half] = part if sums[half] is None else sums[half] + part
        query_valid = (
            lax.broadcasted_iota(jnp.int32, (1, rows), 1) >= valid_first - query_first
        )
        outs = []
        for half in range(2):
            factor = jnp.where(query_valid, 1.0 / sums[half][head_size : head_size + 1], 0.0)
            outs.append(sums[half][:head_size] * factor)
        out_ref[...] = jnp.concatenate(outs, 0).T.astype(out_ref.dtype)

    def key_spec(step, offset):
        return pl.BlockSpec(
            (1, rows, LANES), lambda g, info, win: (info[0] - reach + step, 0, offset + g)
        )

    in_specs = [pl.BlockSpec((rows, LANES), lambda g, info, win: (0, g))]
    in_specs += [key_spec(step, 0) for step in range(steps)]
    in_specs += [key_spec(step, value_first) for step in range(steps)]
    return pl.pallas_call(
        body,
        out_shape=jax.ShapeDtypeStruct((rows, width), jnp.bfloat16),
        grid_spec=pltpu.PrefetchScalarGridSpec(
            num_scalar_prefetch=2,
            grid=(pair_count,),
            in_specs=in_specs,
            out_specs=pl.BlockSpec((rows, LANES), lambda g, info, win: (0, g)),
            scratch_shapes=[pltpu.VMEM((steps, rows, cols), jnp.float32)],
        ),
        cost_estimate=pl.CostEstimate(
            flops=8 * steps * rows * rows * width,
            bytes_accessed=4 * steps * rows * width,
            transcendentals=steps * rows * rows * HEADS,
        ),
        name="attend",
    )(info, head_window, queries, *([buffer] * (2 * steps)))


def on_device(
    history, lengths, head_window, input_proj, output_proj, mixer_down, mixer_up, series_mix
):
    local_series, rows, width = history.shape
    devices = lax.axis_size("tm")
    groups = lax.axis_size("series")
    assert local_series == 2 and devices % 4 == 0 and WINDOW == 2 * rows
    patches = rows * devices
    position = lax.axis_index("tm")
    quad, chip, core = position // 4, (position // 2) % 2, position % 2
    chip_swap, core_swap, near_route, far_route = routes(devices)

    def move(block, route):
        return lax.ppermute(block, "tm", route)

    def part(array, index):
        return lax.dynamic_index_in_dim(array, index, 0, keepdims=False)

    mine = part(history, chip)
    other = part(history, 1 - chip)
    away = move(other, chip_swap)
    near = move(mine, near_route)
    mine_beside = move(mine, core_swap)
    far = move(away, far_route)
    away_beside = move(away, core_swap)
    near_beside = move(near, core_swap)
    far_beside = move(far, core_swap)

    home_slot = 2 + 2 * chip
    away_slot = 4 - 2 * chip
    near_slot = 6 - 6 * chip
    far_slot = 6 * chip

    def slots(*firsts):
        return jnp.stack([f + c for f in firsts for c in (core, 1 - core)]).astype(jnp.int32)

    scale = (width // HEADS) ** (-0.5) * math.log2(math.e)

    def query_rows(block):
        return (
            jnp.dot(block, input_proj[:, :width], preferred_element_type=jnp.float32) * scale
        ).astype(jnp.bfloat16)

    valid_first = patches - part(lengths, chip)

    def attention(slot, queries, buffer):
        query_first = (4 * quad - 2 + slot) * rows
        info = jnp.stack([slot, query_first, valid_first, patches]).astype(jnp.int32)
        return attend(info, head_window, queries, buffer)

    buffer = project([mine, mine_beside], slots(home_slot), input_proj, width, 8)
    buffer = project(
        [away, away_beside, near, near_beside],
        slots(away_slot, near_slot),
        input_proj,
        width,
        8,
        buffer,
    )
    away_out = attention(away_slot + core, query_rows(away), buffer)
    other_attended = move(away_out, chip_swap)
    buffer = project([far, far_beside], slots(far_slot), input_proj, width, 8, buffer)
    mine_attended = attention(home_slot + core, query_rows(mine), buffer)

    def finish(rows_in, attended):
        hidden = (
            rows_in.astype(jnp.float32)
            + jnp.dot(attended, output_proj, preferred_element_type=jnp.float32)
        ).astype(jnp.bfloat16)
        branch = jnp.dot(hidden, mixer_down, preferred_element_type=jnp.float32).astype(
            jnp.bfloat16
        )
        return hidden, branch

    own_group = lax.axis_index("series")

    def from_groups(branch):
        gathered = [branch]
        for shift in range(1, groups):
            route = [((g + shift) % groups, g) for g in range(groups)]
            gathered.append(lax.ppermute(branch, "series", route))
        return gathered

    mine_hidden, mine_branch = finish(mine, mine_attended)
    mine_branches = from_groups(mine_branch)
    other_hidden, other_branch = finish(other, other_attended)
    other_branches = from_groups(other_branch)

    mix = series_mix.astype(jnp.float32)

    def combined(which):
        row = part(mix, own_group * 2 + which)
        total = 0.0
        for shift in range(groups):
            group = (own_group + shift) % groups
            total += part(row, group * 2 + chip) * mine_branches[shift].astype(jnp.float32)
            total += part(row, group * 2 + 1 - chip) * other_branches[shift].astype(jnp.float32)
        return total.astype(jnp.bfloat16)

    def output(hidden, which):
        update = jnp.dot(combined(which), mixer_up, preferred_element_type=jnp.float32)
        return (hidden.astype(jnp.float32) + update).astype(jnp.bfloat16)

    mine_out = output(mine_hidden, chip)
    other_out = output(other_hidden, 1 - chip)
    return jnp.where(
        chip == 0, jnp.stack([mine_out, other_out]), jnp.stack([other_out, mine_out])
    )


def solution(mesh):
    in_specs = (P("series", "tm", None), P("series"), P(), P(), P(), P(), P(), P())
    out_specs = P("series", "tm", None)
    return jax.shard_map(
        on_device, mesh=mesh, in_specs=in_specs, out_specs=out_specs, check_vma=False
    )
```

time: 255 us -> 123 us (0.48)
  local copies, waits for them, and re-layouts: 80 us -> 4.3 us
  Pallas kernels: 0 us -> 64.1 us
  waiting for transfers between devices: 69.8 us -> 14.2 us
  matrix products: 54.1 us -> 20.4 us
  between operations: 13.6 us -> 0.68 us
  loops' own time: 10.8 us -> 0 us
  other arithmetic: 13.6 us -> 4.2 us
  starting transfers between devices: 11.1 us -> 13.8 us
    dynamic_slice x42 -> x2, local copies, waits for them, and re-layouts: 65.9 us -> 1.25 us  [part(): return lax.dynamic_index_in_dim(array, index, 0, keepdims=False)]
    pallas_call x0 -> x5, Pallas kernels: none -> 64.1 us  [the longest x3 32.8 us: project(): pl.pallas_call(body, out_shape=jax.ShapeDtypeStruct((slot_count, rows, co...]
    dot_general x25 -> x8, matrix products: 54.1 us -> 20.4 us  [the longest x2 8.65 us: output(): jnp.dot(combined(which), mixer_up, preferred_element_type=jnp.float32)]
    ppermute x4 -> x10, waiting for transfers between devices: 42.3 us -> 14.2 us  [the longest x2 8.33 us: from_groups(): gathered.append(lax.ppermute(branch, 'series', route))]
    all_gather x1 -> x0, waiting for transfers between devices: 27.6 us -> none  [on_device(): lax.all_gather(branch, 'series', axis=0, tiled=True)]
    another operation x3 -> x0, loops' own time: 10.8 us -> none  [the longest x2 9.47 us: attend_series(): grouped = lax.map(per_group, jnp.arange(group_count, dtype=jnp.int32))]
    reduce_sum x8 -> x0, other arithmetic: 7.71 us -> none  [per_group(): totals = jnp.sum(weights, axis=-1)]
    unnamed x23 -> x18, local copies, waits for them, and re-layouts: 6.82 us -> 0.83 us
  transfers between devices with their start and end apart: 5 -> 10, of which waited for: 2 -> 3; matrix products, arithmetic and copies ran while one was open for 8% -> 13% of each run, Pallas kernels for 0% -> 53%
where the time goes in v1:
time: 123 us; the launch traced here: 122 us
  Pallas kernels  64.1 us (52%)
  matrix products  20.4 us (17%)
  waiting for transfers between devices  14.2 us (12%)
  starting transfers between devices  13.8 us (11%)
  local copies, waits for them, and re-layouts  4.3 us (3%)
  other arithmetic  4.2 us (3%)
    pallas_call x3, Pallas kernels, project(): pl.pallas_call(body, out_shape=jax.ShapeDtypeStruct((slot_count, rows, co...  32.8 us
    pallas_call x2, Pallas kernels, attend(): pl.pallas_call(body, out_shape=jax.ShapeDtypeStruct((rows, width), jnp.bf...  31.4 us
    ppermute x8, starting transfers between devices, move(): return lax.ppermute(block, 'tm', route)  11.7 us
    dot_general x2, matrix products, output(): jnp.dot(combined(which), mixer_up, preferred_element_type=jnp.float32)  8.65 us
    ppermute x2, waiting for transfers between devices, from_groups(): gathered.append(lax.ppermute(branch, 'series', route))  8.33 us
    dot_general x2, matrix products, query_rows(): jnp.dot(block, input_proj[:, :width], preferred_element_type=jnp.float32)  6.41 us
    ppermute x8, waiting for transfers between devices, move(): return lax.ppermute(block, 'tm', route)  5.92 us
    dot_general x2, matrix products, finish(): jnp.dot(attended, output_proj, preferred_element_type=jnp.float32)  3.75 us
  transfers between devices with their start and end apart: 10, of which 3 were waited for; matrix products, arithmetic and copies ran while one was open for 13% of the time, Pallas kernels for 53%

profile of v1, /device:TPU:0, one launch (start us, length us, event | category | flops | bytes accessed | tf_op | source)
XLA Modules:
  0.0 121.8 jit_solution(2841874666072657032)
XLA Ops:
  0.0 2.2 %dynamic-slice_bitcast_fusion.1 = (bf16[256,1024]{1,0:T(8,128)(2,1)S(1)}, bf16[256,1024]{1,0:T(8,128)(2,1)}) fusion(bf16[2,256,1024]{2,1,0:T(8,128)(2,1)} %param.8, s32[]{:T(128)S(6)} %select_n.86, s32[]{:T(128)S(6)} %select_n.89), kind=kLoop, calls=%fused_computation.37 | loop fusion | bytes 2097160 | tf_op jit(solution)/shard_map/jit(dynamic_index_in_dim)/squeeze | solution.py:197
  2.2 0.5 collective-permute-start.6
  2.7 1.3 %collective-permute-start.4 = (bf16[256,1024]{1,0:T(8,128)(2,1)S(1)}, bf16[256,1024]{1,0:T(8,128)(2,1)S(1)}, u32[]{:S(2)}, u32[]{:S(2)}) collective-permute-start(bf16[256,1024]{1,0:T(8,128)(2,1)S(1)} %get-tuple-element.5.refs_0_), channel_id=1, source_target_pairs={{4,12},{6,14},{8,0},{10,2},{12,20},{14,22},{16,8},{18,10},{20,28},... | collective-permute-start | bytes 1572872 | tf_op jit(solution)/shard_map/ppermute | solution.py:194
  4.0 4.8 %collective-permute-start = (bf16[256,1024]{1,0:T(8,128)(2,1)}, bf16[256,1024]{1,0:T(8,128)(2,1)}, u32[]{:S(2)}, u32[]{:S(2)}) collective-permute-start(bf16[256,1024]{1,0:T(8,128)(2,1)} %get-tuple-element.6), channel_id=1, source_target_pairs={{0,4},{2,6},{4,0},{6,2},{8,12},{10,14},{12,8},{14,10},{16,20},{18,... | collective-permute-start | bytes 1572872 | tf_op jit(solution)/shard_map/ppermute | solution.py:194
  8.8 0.6 dynamic_slice.40
  9.4 0.6 pad_add_fusion.4.slots_ref
  10.6 0.6 pad_add_fusion.1.info_ref
  11.2 0.6 pad_add_fusion.info_ref
  11.8 0.6 pad_add_fusion.2.slots_ref
  12.4 3.1 %fusion.16.query_ref = bf16[256,1024]{1,0:T(8,128)(2,1)} fusion(bf16[256,1024]{1,0:T(8,128)(2,1)S(1)} %get-tuple-element.5.refs_0_, bf16[1024,3072]{1,0:T(8,128)(2,1)} %refs_2_.3), kind=kOutput, calls=%fused_computation.13 | convolution fusion | flops 537395200 | bytes 3145728 | tf_op jit(solution)/shard_map/dot_general | solution.py:221
  15.5 5.9 %collective-permute-done.refs_0_ = bf16[256,1024]{1,0:T(8,128)(2,1)} collective-permute-done((bf16[256,1024]{1,0:T(8,128)(2,1)}, bf16[256,1024]{1,0:T(8,128)(2,1)}, u32[]{:S(2)}, u32[]{:S(2)}) %collective-permute-start) | collective-permute-done | bytes 524320 | tf_op jit(solution)/shard_map/ppermute | solution.py:194
  21.4 4.2 %collective-permute-start.1 = (bf16[256,1024]{1,0:T(8,128)(2,1)}, bf16[256,1024]{1,0:T(8,128)(2,1)}, u32[]{:S(2)}, u32[]{:S(2)}) collective-permute-start(bf16[256,1024]{1,0:T(8,128)(2,1)} %collective-permute-done.refs_0_), channel_id=1, source_target_pairs={{0,8},{2,10},{8,16},{10,18},{12,4},{14,6},{16,24},{18,26},{20,12},... | collective-permute-start | bytes 1572872 | tf_op jit(solution)/shard_map/ppermute | solution.py:194
  25.9 0.6 pad_add_fusion.3.slots_ref
  26.5 9.2 %project.3.refs_5_ = bf16[8,256,2048]{2,1,0:T(8,128)(2,1)} custom-call(s32[2]{0:T(128)} %pad_add_fusion.4.slots_ref, bf16[256,1024]{1,0:T(8,128)(2,1)} %copy-done.2, bf16[256,1024]{1,0:T(8,128)(2,1)} %collective-permute-done.6.refs_1_, bf16[1024,3072]{1,0:T(8,128)(2,1)} %refs_2_.3), custom_call_target="tpu_custom_call" | custom-call | flops 2147483648 | bytes 4194304 | tf_op jit(solution)/shard_map/project/pallas_call | solution.py:63
  35.8 3.3 %fusion.13.query_ref = bf16[256,1024]{1,0:T(8,128)(2,1)} fusion(bf16[256,1024]{1,0:T(8,128)(2,1)} %collective-permute-done.refs_0_, bf16[1024,3072]{1,0:T(8,128)(2,1)} %refs_2_.3), kind=kOutput, calls=%fused_computation.12 | convolution fusion | flops 537395200 | bytes 3145728 | tf_op jit(solution)/shard_map/dot_general | solution.py:221
  39.3 14.3 %project.4.refs_3_.refs_0_.refs_1_.refs_2_.refs_4_.refs_5_.refs_6_.refs_7_.refs_8_.refs_9_ = bf16[8,256,2048]{2,1,0:T(8,128)(2,1)} custom-call(s32[4]{0:T(128)} %pad_add_fusion.3.slots_ref, bf16[256,1024]{1,0:T(8,128)(2,1)} %collective-permute-done.refs_0_, bf16[256,1024]{1,0:T(8,128)(2,1)} %collective-permute-done.3.refs_1_, ...), custom_call_target="tpu_custom_call", output_to_operand_aliasing={{}: (6, {})} | custom-call | flops 4294967296 | bytes 4194304 | tf_op jit(solution)/shard_map/project/pallas_call | solution.py:63
  53.6 15.6 %attend.3 = bf16[256,1024]{1,0:T(8,128)(2,1)} custom-call(s32[4]{0:T(128)} %pad_add_fusion.info_ref, s32[16]{0:T(128)} %window_ref.3, bf16[256,1024]{1,0:T(8,128)(2,1)} %fusion.13.query_ref, bf16[8,256,2048]{2,1,0:T(8,128)(2,1)} %project.4.refs_3_.refs_0_.refs_1_.refs_2_.refs_4_.refs_5_.refs_6_.refs_7_.refs_8_.refs_9_, ...), custom_call_target="tpu_custom_call" | custom-call | flops 2684354560 | bytes 5242880 | tf_op jit(solution)/shard_map/attend/pallas_call | solution.py:162
  69.7 0.8 copy-done.5
  70.5 9.2 %project.5.refs_0_.refs_1_.refs_2_.refs_3_.refs_4_.refs_5_.refs_6_.refs_7_.refs_8_.refs_9_ = bf16[8,256,2048]{2,1,0:T(8,128)(2,1)} custom-call(s32[2]{0:T(128)} %pad_add_fusion.2.slots_ref, bf16[256,1024]{1,0:T(8,128)(2,1)} %collective-permute-done.1.refs_0_, bf16[256,1024]{1,0:T(8,128)(2,1)} %copy-done.5, ...), custom_call_target="tpu_custom_call", output_to_operand_aliasing={{}: (4, {})} | custom-call | flops 2147483648 | bytes 4194304 | tf_op jit(solution)/shard_map/project/pallas_call | solution.py:63
  79.7 15.8 %attend.2 = bf16[256,1024]{1,0:T(8,128)(2,1)} custom-call(s32[4]{0:T(128)} %pad_add_fusion.1.info_ref, s32[16]{0:T(128)} %window_ref.3, bf16[256,1024]{1,0:T(8,128)(2,1)} %fusion.16.query_ref, bf16[8,256,2048]{2,1,0:T(8,128)(2,1)} %project.5.refs_0_.refs_1_.refs_2_.refs_3_.refs_4_.refs_5_.refs_6_.refs_7_.refs_8_.refs_9_, ...), custom_call_target="tpu_custom_call" | custom-call | flops 2684354560 | bytes 5242880 | tf_op jit(solution)/shard_map/attend/pallas_call | solution.py:162
  95.5 1.8 %fusion.11 = bf16[256,1024]{1,0:T(8,128)(2,1)S(1)} fusion(bf16[256,1024]{1,0:T(8,128)(2,1)} %attend.2, bf16[1024,1024]{1,0:T(8,128)(2,1)S(1)} %copy-done, bf16[256,1024]{1,0:T(8,128)(2,1)S(1)} %copy-done.3), kind=kOutput, calls=%fused_computation.10 | convolution fusion | flops 537657344 | bytes 3670016 | tf_op jit(solution)/shard_map/dot_general | solution.py:248
  97.4 0.4 convolution_convert_fusion.1
  97.8 1.6 %collective-permute-start.8 = (bf16[256,512]{1,0:T(8,128)(2,1)S(1)}, bf16[256,512]{1,0:T(8,128)(2,1)}, u32[]{:S(2)}, u32[]{:S(2)}) collective-permute-start(bf16[256,512]{1,0:T(8,128)(2,1)S(1)} %convolution_convert_fusion.1), channel_id=1, source_target_pairs={{1,0},{0,1},{3,2},{2,3},{5,4},{4,5},{7,6},{6,7},{9,8},{8,9},{11,10... | collective-permute-start | bytes 786440 | tf_op jit(solution)/shard_map/ppermute | solution.py:261
  99.4 1.9 %fusion.12 = bf16[256,1024]{1,0:T(8,128)(2,1)S(1)} fusion(bf16[256,1024]{1,0:T(8,128)(2,1)} %collective-permute-done.7, bf16[1024,1024]{1,0:T(8,128)(2,1)S(1)} %copy-done, bf16[256,1024]{1,0:T(8,128)(2,1)} %get-tuple-element.6), kind=kOutput, calls=%fused_computation.11 | convolution fusion | flops 537657344 | bytes 3670016 | tf_op jit(solution)/shard_map/dot_general | solution.py:248
  101.3 1.1 convolution_convert_fusion
  102.4 0.5 collective-permute-start.9
  103.0 0.7 fusion.42
  103.6 3.5 %collective-permute-done.8 = bf16[256,512]{1,0:T(8,128)(2,1)} collective-permute-done((bf16[256,512]{1,0:T(8,128)(2,1)S(1)}, bf16[256,512]{1,0:T(8,128)(2,1)}, u32[]{:S(2)}, u32[]{:S(2)}) %collective-permute-start.8) | collective-permute-done | bytes 262176 | tf_op jit(solution)/shard_map/ppermute | solution.py:261
  107.2 4.8 %collective-permute-done.9 = bf16[256,512]{1,0:T(8,128)(2,1)} collective-permute-done((bf16[256,512]{1,0:T(8,128)(2,1)}, bf16[256,512]{1,0:T(8,128)(2,1)}, u32[]{:S(2)}, u32[]{:S(2)}) %collective-permute-start.9) | collective-permute-done | bytes 262176 | tf_op jit(solution)/shard_map/ppermute | solution.py:261
  112.0 4.6 %fusion.19 = bf16[1,256,1024]{2,1,0:T(8,128)(2,1)S(1)} fusion(bf16[512,1024]{1,0:T(8,128)(2,1)} %param.14, bf16[256,1024]{1,0:T(8,128)(2,1)S(1)} %fusion.11, bf16[256,512]{1,0:T(8,128)(2,1)S(1)} %convolution_convert_fusion.1, bf16[256,512]{1,0:T(8,128)(2,1)} %convolution_convert_fusion, bf16[256,512]{1,0:T(8,128)(2,1)} %collective-permute-done.8, ...), kind=kOutput, calls=%fused_computation.14 | convolution fusion | flops 270794752 | bytes 3145744 | tf_op jit(solution)/shard_map/dot_general | solution.py:281
  116.6 4.1 %fusion.28 = bf16[1,256,1024]{2,1,0:T(8,128)(2,1)S(1)} fusion(bf16[256,1024]{1,0:T(8,128)(2,1)S(1)} %fusion.12, bf16[512,1024]{1,0:T(8,128)(2,1)S(1)} %copy-done.7, bf16[256,512]{1,0:T(8,128)(2,1)S(1)} %convolution_convert_fusion.1, bf16[256,512]{1,0:T(8,128)(2,1)} %convolution_convert_fusion, bf16[256,512]{1,0:T(8,128)(2,1)} %collective-permute-done.8, ...), kind=kOutput, calls=%fused_computation.35 | convolution fusion | flops 270794752 | bytes 3145744 | tf_op jit(solution)/shard_map/dot_general | solution.py:281
  120.6 1.1 maximum_select_fusion
  (28 shorter events, 1.0 us)
Async XLA Ops:
  0.0 95.5 %copy-start = (bf16[1024,1024]{1,0:T(8,128)(2,1)S(1)}, bf16[1024,1024]{1,0:T(8,128)(2,1)}, u32[]{:S(2)}) copy-start(bf16[1024,1024]{1,0:T(8,128)(2,1)} %param.12) | copy-start | bytes 6291460
  0.0 8.8 %copy-start.8 = (s32[2]{0:T(128)S(1)}, s32[2]{0:T(128)}, u32[]{:S(2)}) copy-start(s32[2]{0:T(128)} %param.9) | copy-start | bytes 28
  2.2 13.3 %copy-start.2 = (bf16[256,1024]{1,0:T(8,128)(2,1)}, bf16[256,1024]{1,0:T(8,128)(2,1)S(1)}, u32[]{:S(2)}) copy-start(bf16[256,1024]{1,0:T(8,128)(2,1)S(1)} %get-tuple-element.5.refs_0_) | copy-start | bytes 1572868
  2.2 24.3 %collective-permute-start.6 = (bf16[256,1024]{1,0:T(8,128)(2,1)S(1)}, bf16[256,1024]{1,0:T(8,128)(2,1)}, u32[]{:S(2)}, u32[]{:S(2)}) collective-permute-start(bf16[256,1024]{1,0:T(8,128)(2,1)S(1)} %get-tuple-element.5.refs_0_), channel_id=1, source_target_pairs={{0,2},{2,0},{4,6},{6,4},{8,10},{10,8},{12,14},{14,12},{16,18},{18,... | collective-permute-start | bytes 1572872 | tf_op jit(solution)/shard_map/ppermute | solution.py:194
  2.7 23.0 %collective-permute-start.4 = (bf16[256,1024]{1,0:T(8,128)(2,1)S(1)}, bf16[256,1024]{1,0:T(8,128)(2,1)S(1)}, u32[]{:S(2)}, u32[]{:S(2)}) collective-permute-start(bf16[256,1024]{1,0:T(8,128)(2,1)S(1)} %get-tuple-element.5.refs_0_), channel_id=1, source_target_pairs={{4,12},{6,14},{8,0},{10,2},{12,20},{14,22},{16,8},{18,10},{20,28},... | collective-permute-start | bytes 1572872 | tf_op jit(solution)/shard_map/ppermute | solution.py:194
  4.0 17.4 %collective-permute-start = (bf16[256,1024]{1,0:T(8,128)(2,1)}, bf16[256,1024]{1,0:T(8,128)(2,1)}, u32[]{:S(2)}, u32[]{:S(2)}) collective-permute-start(bf16[256,1024]{1,0:T(8,128)(2,1)} %get-tuple-element.6), channel_id=1, source_target_pairs={{0,4},{2,6},{4,0},{6,2},{8,12},{10,14},{12,8},{14,10},{16,20},{18,... | collective-permute-start | bytes 1572872 | tf_op jit(solution)/shard_map/ppermute | solution.py:194
  21.4 17.9 %collective-permute-start.3 = (bf16[256,1024]{1,0:T(8,128)(2,1)}, bf16[256,1024]{1,0:T(8,128)(2,1)}, u32[]{:S(2)}, u32[]{:S(2)}) collective-permute-start(bf16[256,1024]{1,0:T(8,128)(2,1)} %collective-permute-done.refs_0_), channel_id=1, source_target_pairs={{0,2},{2,0},{4,6},{6,4},{8,10},{10,8},{12,14},{14,12},{16,18},{18,... | collective-permute-start | bytes 1572872 | tf_op jit(solution)/shard_map/ppermute | solution.py:194
  21.4 17.6 %collective-permute-start.1 = (bf16[256,1024]{1,0:T(8,128)(2,1)}, bf16[256,1024]{1,0:T(8,128)(2,1)}, u32[]{:S(2)}, u32[]{:S(2)}) collective-permute-start(bf16[256,1024]{1,0:T(8,128)(2,1)} %collective-permute-done.refs_0_), channel_id=1, source_target_pairs={{0,8},{2,10},{8,16},{10,18},{12,4},{14,6},{16,24},{18,26},{20,12},... | collective-permute-start | bytes 1572872 | tf_op jit(solution)/shard_map/ppermute | solution.py:194
  25.7 10.1 %copy-start.4 = (bf16[256,1024]{1,0:T(8,128)(2,1)}, bf16[256,1024]{1,0:T(8,128)(2,1)S(1)}, u32[]{:S(2)}) copy-start(bf16[256,1024]{1,0:T(8,128)(2,1)S(1)} %collective-permute-done.4.refs_2_) | copy-start | bytes 1572868
  25.7 13.6 %collective-permute-start.5 = (bf16[256,1024]{1,0:T(8,128)(2,1)S(1)}, bf16[256,1024]{1,0:T(8,128)(2,1)}, u32[]{:S(2)}, u32[]{:S(2)}) collective-permute-start(bf16[256,1024]{1,0:T(8,128)(2,1)S(1)} %collective-permute-done.4.refs_2_), channel_id=1, source_target_pairs={{0,2},{2,0},{4,6},{6,4},{8,10},{10,8},{12,14},{14,12},{16,18},{18,... | collective-permute-start | bytes 1572872 | tf_op jit(solution)/shard_map/ppermute | solution.py:194
  39.1 30.6 %collective-permute-start.2 = (bf16[256,1024]{1,0:T(8,128)(2,1)}, bf16[256,1024]{1,0:T(8,128)(2,1)S(1)}, u32[]{:S(2)}, u32[]{:S(2)}) collective-permute-start(bf16[256,1024]{1,0:T(8,128)(2,1)} %collective-permute-done.1.refs_0_), channel_id=1, source_target_pairs={{0,2},{2,0},{4,6},{6,4},{8,10},{10,8},{12,14},{14,12},{16,18},{18,... | collective-permute-start | bytes 1572872 | tf_op jit(solution)/shard_map/ppermute | solution.py:194
  69.2 30.1 %collective-permute-start.7 = (bf16[256,1024]{1,0:T(8,128)(2,1)}, bf16[256,1024]{1,0:T(8,128)(2,1)}, u32[]{:S(2)}, u32[]{:S(2)}) collective-permute-start(bf16[256,1024]{1,0:T(8,128)(2,1)} %attend.3), channel_id=1, source_target_pairs={{0,4},{2,6},{4,0},{6,2},{8,12},{10,14},{12,8},{14,10},{16,20},{18,... | collective-permute-start | bytes 1572872 | tf_op jit(solution)/shard_map/ppermute | solution.py:194
  69.7 0.8 copy-start.5
  79.7 15.8 %copy-start.3 = (bf16[256,1024]{1,0:T(8,128)(2,1)S(1)}, bf16[256,1024]{1,0:T(8,128)(2,1)}, u32[]{:S(2)}) copy-start(bf16[256,1024]{1,0:T(8,128)(2,1)} %copy-done.2) | copy-start | bytes 1572868
  95.5 1.9 %copy-start.1 = (bf16[1024,512]{1,0:T(8,128)(2,1)S(1)}, bf16[1024,512]{1,0:T(8,128)(2,1)}, u32[]{:S(2)}) copy-start(bf16[1024,512]{1,0:T(8,128)(2,1)} %param.13) | copy-start | bytes 3145732
  97.8 5.2 %copy-start.6 = (bf16[4,4]{1,0:T(4,128)(2,1)S(1)}, bf16[4,4]{1,0:T(4,128)(2,1)}, u32[]{:S(2)}) copy-start(bf16[4,4]{1,0:T(4,128)(2,1)} %param.15) | copy-start | bytes 100
  97.8 9.3 %collective-permute-start.8 = (bf16[256,512]{1,0:T(8,128)(2,1)S(1)}, bf16[256,512]{1,0:T(8,128)(2,1)}, u32[]{:S(2)}, u32[]{:S(2)}) collective-permute-start(bf16[256,512]{1,0:T(8,128)(2,1)S(1)} %convolution_convert_fusion.1), channel_id=1, source_target_pairs={{1,0},{0,1},{3,2},{2,3},{5,4},{4,5},{7,6},{6,7},{9,8},{8,9},{11,10... | collective-permute-start | bytes 786440 | tf_op jit(solution)/shard_map/ppermute | solution.py:261
  102.4 9.5 %collective-permute-start.9 = (bf16[256,512]{1,0:T(8,128)(2,1)}, bf16[256,512]{1,0:T(8,128)(2,1)}, u32[]{:S(2)}, u32[]{:S(2)}) collective-permute-start(bf16[256,512]{1,0:T(8,128)(2,1)} %convolution_convert_fusion), channel_id=1, source_target_pairs={{1,0},{0,1},{3,2},{2,3},{5,4},{4,5},{7,6},{6,7},{9,8},{8,9},{11,10... | collective-permute-start | bytes 786440 | tf_op jit(solution)/shard_map/ppermute | solution.py:261
  103.0 13.6 %copy-start.7 = (bf16[512,1024]{1,0:T(8,128)(2,1)S(1)}, bf16[512,1024]{1,0:T(8,128)(2,1)}, u32[]{:S(2)}) copy-start(bf16[512,1024]{1,0:T(8,128)(2,1)} %param.14) | copy-start | bytes 3145732

commit v2 on v1

v2 whole, which is shorter than its diff:
```python
import functools
import math

import jax
import jax.numpy as jnp
from jax import lax
from jax.experimental import pallas as pl
from jax.experimental.pallas import tpu as pltpu
from jax.sharding import PartitionSpec as P

HEADS = 16
WINDOW = 512
LANES = 128
MASKED = -1e30


def routes(count):
    place = lambda quad, chip, core: 4 * quad + 2 * chip + core
    last = count // 4 - 1
    chip_swap = [(i, i ^ 2) for i in range(count)]
    core_swap = [(i, i ^ 1) for i in range(count)]
    near, far = [], []
    for i in range(count):
        quad, chip, core = i // 4, (i // 2) % 2, i % 2
        down = quad - 1 if quad > 0 else None
        up = quad + 1 if quad < last else None
        near_quad, far_quad = (down, up) if chip == 0 else (up, down)
        if near_quad is not None:
            near.append((i, place(near_quad, chip, core)))
        if far_quad is not None:
            far.append((i, place(far_quad, chip, core)))
    return chip_swap, core_swap, near, far


def project(first, beside, weight, scale):
    rows, width = first.shape
    chunk = min(256, width)
    steps = width // chunk

    def body(first_ref, beside_ref, wq_ref, wk_ref, wv_ref, q_ref, k_ref, v_ref):
        def dot(block, ref):
            return jnp.dot(block[...], ref[...], preferred_element_type=jnp.float32)

        q_ref[...] = (dot(first_ref, wq_ref) * scale).astype(jnp.bfloat16)
        for index, block in enumerate((first_ref, beside_ref)):
            k_ref[index] = dot(block, wk_ref).astype(jnp.bfloat16)
            v_ref[index] = dot(block, wv_ref).astype(jnp.bfloat16).T

    whole = pl.BlockSpec((rows, width), lambda g: (0, 0))
    weights = [
        pl.BlockSpec((width, chunk), lambda g, part=part: (0, part * steps + g))
        for part in range(3)
    ]
    return pl.pallas_call(
        body,
        out_shape=(
            jax.ShapeDtypeStruct((rows, width), jnp.bfloat16),
            jax.ShapeDtypeStruct((2, rows, width), jnp.bfloat16),
            jax.ShapeDtypeStruct((2, width, rows), jnp.bfloat16),
        ),
        grid=(steps,),
        in_specs=[whole, whole] + weights,
        out_specs=(
            pl.BlockSpec((rows, chunk), lambda g: (0, g)),
            pl.BlockSpec((2, rows, chunk), lambda g: (0, 0, g)),
            pl.BlockSpec((2, chunk, rows), lambda g: (0, g, 0)),
        ),
        cost_estimate=pl.CostEstimate(
            flops=10 * rows * width * width, bytes_accessed=6 * width * width, transcendentals=0
        ),
        name="project",
    )(first, beside, weight, weight, weight)


def attend(place, head_window, lengths, weight, scale, home, raw, ready, queries=None, keep=0):
    raw_sides = [side for side, _ in raw]
    ready_sides = [side for side, _ in ready]
    raw = [block for _, blocks in raw for block in blocks]
    ready = [arrays for _, arrays in ready]
    rows, width = raw[0].shape
    devices = lax.axis_size("tm")
    head_size = width // HEADS
    pairs = width // LANES
    reach = WINDOW // rows
    steps = 2 * reach + 1
    slot_count = steps + 1
    half_rows = rows // 2
    cols = 2 * half_rows
    raw_count, ready_count = len(raw), len(ready)

    def span(step, half):
        if step == 0 and half == 1:
            return half_rows, rows
        if step == steps - 1 and half == 0:
            return 0, half_rows
        return 0, rows

    def body(place_ref, window_ref, length_ref, *refs):
        refs = list(refs)
        take = lambda count: [refs.pop(0) for _ in range(count)]
        raw_refs = take(raw_count)
        ready_refs = take(2 * ready_count)
        query_ref = take(1)[0] if queries is not None else None
        wq_ref = take(1)[0] if queries is None else None
        wk_ref, wv_ref, out_ref = take(3)
        keep_refs = take(2) if keep else None
        key_scr, weight_scr, row_scr, query_scr = take(4)
        value_scrs, score_scrs, top_scrs = take(2), take(2), take(2)
        index = pl.program_id(0)
        position = place_ref[0]
        core = position % 2
        chip = (position // 2) % 2
        patches = rows * devices
        valid_first = patches - length_ref[chip]
        query_chip = chip if home else 1 - chip
        query_first = (position - 2 * chip + 2 * query_chip) * rows

        def slot_of(side, beside):
            offset = core if not beside else 1 - core
            return 2 + 2 * side * (1 - 2 * chip) + offset

        @pl.when(index == 0)
        def _():
            row_scr[...] = lax.broadcasted_iota(jnp.int32, (rows, LANES), 0)

        def front(parity, value_scr, score_scr, top_scr):
            units = []
            state = {}

            def ready_blocks():
                for number in range(ready_count):
                    for which in range(2):
                        slot = slot_of(ready_sides[number], which)
                        key_scr[slot] = ready_refs[2 * number][which]
                        value_scr[slot] = ready_refs[2 * number + 1][which]
                weight_scr[:, :LANES] = wk_ref[...]
                weight_scr[:, LANES:] = wv_ref[...]

            units.append(ready_blocks)

            def project_queries():
                both = jnp.dot(raw_refs[0][...], wq_ref[...], preferred_element_type=jnp.float32)
                query_scr[...] = (both * scale).astype(jnp.bfloat16)

            if query_ref is None and parity == 0:
                units.append(project_queries)

            def project_block(number, part):
                slot = slot_of(raw_sides[number // 2], number % 2)
                where = slice(part * half_rows, (part + 1) * half_rows)
                both = jnp.dot(
                    raw_refs[number][where, :], weight_scr[...], preferred_element_type=jnp.float32
                ).astype(jnp.bfloat16)
                keys, values = both[:, :LANES], both[:, LANES:].T
                key_scr[slot, where, :] = keys
                value_scr[slot, :, where] = values
                if number < keep:
                    keep_refs[0][number, where, :] = keys
                    keep_refs[1][number, :, where] = values

            for number in range(raw_count):
                for part in range(2):
                    units.append(functools.partial(project_block, number, part))
            early = len(units)

            def bounds(half):
                column = lax.broadcasted_iota(jnp.int32, (1, cols), 1)
                second = column >= half_rows
                window = jnp.where(second, window_ref[2 * index + 1], window_ref[2 * index])
                lane = lax.broadcasted_iota(jnp.int32, (half_rows, LANES), 1)
                local = jnp.where(second, column - half_rows, column) + half * half_rows
                lowest = jnp.maximum(local - window, valid_first - query_first)
                highest = jnp.minimum(local + window, patches - 1 - query_first)
                where = slice(half * half_rows, (half + 1) * half_rows)
                if query_ref is None:
                    part = query_scr[where, parity * LANES : (parity + 1) * LANES]
                else:
                    part = query_ref[where, :]
                zero = jnp.zeros_like(part)
                right = jnp.concatenate(
                    [
                        jnp.where(lane < head_size, part, zero),
                        jnp.where(lane < head_size, zero, part),
                    ],
                    0,
                )
                return right, lowest, highest

            def score_block(half, step):
                if step == 0:
                    state[half] = bounds(half)
                right, lowest, highest = state[half]
                start, stop = span(step, half)
                first = (step - reach) * rows
                scores = lax.dot_general(
                    key_scr[core + step, start:stop, :],
                    right,
                    (((1,), (1,)), ((), ())),
                    preferred_element_type=jnp.float32,
                )
                key_row = row_scr[start:stop, :]
                key_row = jnp.concatenate([key_row] * (cols // LANES), 1)
                allowed = None
                if step <= reach:
                    allowed = key_row >= lowest - first
                if step >= reach:
                    upper = key_row <= highest - first
                    allowed = upper if allowed is None else allowed & upper
                scores = jnp.where(allowed, scores, MASKED)
                score_scr[half, step, start:stop, :] = scores
                top = jnp.max(scores, axis=0, keepdims=True)
                if step > 0:
                    top = jnp.maximum(state["top"], top)
                state["top"] = top
                if step == steps - 1:
                    top_scr[half] = top

            for half in range(2):
                for step in range(steps):
                    units.append(functools.partial(score_block, half, step))
            return units[:early], units[early:]

        def back(value_scr, score_scr, top_scr):
            sums = [None, None]

            def add_block(step, head):
                where = slice(head * half_rows, (head + 1) * half_rows)
                parts = []
                for half in range(2):
                    start, stop = span(step, half)
                    part = jnp.exp2(
                        score_scr[half, step, start:stop, where] - top_scr[half][:, where]
                    )
                    part = [part.astype(jnp.bfloat16)]
                    if start > 0:
                        part = [jnp.zeros((start, half_rows), jnp.bfloat16)] + part
                    if stop < rows:
                        part = part + [jnp.zeros((rows - stop, half_rows), jnp.bfloat16)]
                    parts.append(jnp.concatenate(part, 0) if len(part) > 1 else part[0])
                weights = jnp.concatenate(parts, 1)
                left = jnp.concatenate(
                    [
                        value_scr[core + step, head * head_size : (head + 1) * head_size, :],
                        jnp.ones((16, rows), jnp.bfloat16),
                    ],
                    0,
                )
                add = jnp.dot(left, weights, preferred_element_type=jnp.float32)
                sums[head] = add if sums[head] is None else sums[head] + add

            def write():
                query_valid = (
                    lax.broadcasted_iota(jnp.int32, (1, rows), 1) >= valid_first - query_first
                )
                outs = []
                for head in range(2):
                    total = sums[head][head_size : head_size + 1]
                    factor = jnp.where(query_valid, 1.0 / total, 0.0)
                    outs.append(sums[head][:head_size] * factor)
                out_ref[...] = jnp.concatenate(outs, 0).T.astype(out_ref.dtype)

            units = [
                functools.partial(add_block, step, head)
                for head in range(2)
                for step in range(steps)
            ]
            return units + [write]

        def interleave(first, second):
            done = 0
            for number, unit in enumerate(first):
                unit()
                target = (number + 1) * len(second) // len(first)
                for other in second[done:target]:
                    other()
                done = target

        sets = [(value_scrs[n], score_scrs[n], top_scrs[n]) for n in range(2)]
        for parity in range(2):

            @pl.when((index < pairs) & (index % 2 == parity))
            def _():
                early, late = front(parity, *sets[parity])
                interleave(early, back(*sets[1 - parity]))
                interleave(late, [])

        @pl.when(index == pairs)
        def _():
            for unit in back(*sets[(pairs - 1) % 2]):
                unit()

    ahead = lambda g: jnp.minimum(g, pairs - 1)
    block = pl.BlockSpec((rows, LANES), lambda g, *_: (0, ahead(g)))
    key_spec = lambda count: pl.BlockSpec((count, rows, LANES), lambda g, *_: (0, 0, ahead(g)))
    value_spec = lambda count: pl.BlockSpec((count, LANES, rows), lambda g, *_: (0, ahead(g), 0))
    weight_spec = lambda part: pl.BlockSpec(
        (width, LANES), lambda g, *_: (0, part * pairs + ahead(g))
    )
    in_specs = [pl.BlockSpec((rows, width), lambda g, *_: (0, 0)) for _ in raw]
    operands = list(raw)
    for keys, values in ready:
        in_specs += [key_spec(2), value_spec(2)]
        operands += [keys, values]
    if queries is not None:
        in_specs.append(block)
        operands.append(queries)
    else:
        in_specs.append(
            pl.BlockSpec((width, 2 * LANES), lambda g, *_: (0, ahead(g) // 2))
        )
        operands.append(weight)
    in_specs += [weight_spec(1), weight_spec(2)]
    operands += [weight, weight]
    out_shape = [jax.ShapeDtypeStruct((rows, width), jnp.bfloat16)]
    out_specs = [pl.BlockSpec((rows, LANES), lambda g, *_: (0, jnp.maximum(g - 1, 0)))]
    if keep:
        out_shape += [
            jax.ShapeDtypeStruct((keep, rows, width), jnp.bfloat16),
            jax.ShapeDtypeStruct((keep, width, rows), jnp.bfloat16),
        ]
        out_specs += [key_spec(keep), value_spec(keep)]
    twice = lambda shape, dtype: [pltpu.VMEM(shape, dtype)] * 2
    return pl.pallas_call(
        body,
        out_shape=tuple(out_shape),
        grid_spec=pltpu.PrefetchScalarGridSpec(
            num_scalar_prefetch=3,
            grid=(pairs + 1,),
            in_specs=in_specs,
            out_specs=tuple(out_specs),
            scratch_shapes=[
                pltpu.VMEM((slot_count, rows, LANES), jnp.bfloat16),
                pltpu.VMEM((width, 2 * LANES), jnp.bfloat16),
                pltpu.VMEM((rows, LANES), jnp.int32),
                pltpu.VMEM((rows, 2 * LANES), jnp.bfloat16),
            ]
            + twice((slot_count, LANES, rows), jnp.bfloat16)
            + twice((2, steps, rows, cols), jnp.float32)
            + twice((2, 1, cols), jnp.float32),
        ),
        cost_estimate=pl.CostEstimate(
            flops=(8 * steps * rows + 4 * raw_count * width) * rows * width,
            bytes_accessed=4 * width * width + 4 * steps * rows * width,
            transcendentals=steps * rows * rows * HEADS,
        ),
        name="attend",
    )(place, head_window, lengths, *operands)


def mix(place, own_group, series_mix, weight, hidden, branches):
    rows, width = hidden[0].shape
    inner = weight.shape[0]
    groups = len(branches[0])

    def body(place_ref, group_ref, mix_ref, weight_ref, *refs):
        hidden_refs = refs[:2]
        branch_refs = refs[2 : 2 + 2 * groups]
        out_ref = refs[-1]
        own = group_ref[0]
        chip = (place_ref[0] // 2) % 2
        for which in range(2):

            @pl.when(pl.program_id(0) == which)
            def _():
                series = [chip, 1 - chip]
                row = 2 * own + series[which]
                total = None
                for number, branch_ref in enumerate(branch_refs):
                    kind, shift = number // groups, number % groups
                    group = (own + shift) % groups
                    term = mix_ref[row, 2 * group + series[kind]] * branch_ref[...].astype(
                        jnp.float32
                    )
                    total = term if total is None else total + term
                update = jnp.dot(
                    total.astype(jnp.bfloat16), weight_ref[...], preferred_element_type=jnp.float32
                )
                out_ref[0] = (hidden_refs[which][...].astype(jnp.float32) + update).astype(
                    out_ref.dtype
                )

    def out_index(which, place_ref, *_):
        chip = (place_ref[0] // 2) % 2
        return chip + which - 2 * chip * which, 0, 0

    whole = lambda shape: pl.BlockSpec(shape, lambda which, *_: (0, 0))
    return pl.pallas_call(
        body,
        out_shape=jax.ShapeDtypeStruct((2, rows, width), jnp.bfloat16),
        grid_spec=pltpu.PrefetchScalarGridSpec(
            num_scalar_prefetch=3,
            grid=(2,),
            in_specs=[whole((inner, width))]
            + [whole((rows, width))] * 2
            + [whole((rows, inner))] * (2 * groups),
            out_specs=pl.BlockSpec((1, rows, width), out_index),
        ),
        cost_estimate=pl.CostEstimate(
            flops=4 * rows * inner * width, bytes_accessed=2 * inner * width, transcendentals=0
        ),
        name="mix",
    )(place, own_group, series_mix, weight, *hidden, *branches[0], *branches[1])


def on_device(
    history, lengths, head_window, input_proj, output_proj, mixer_down, mixer_up, series_mix
):
    local_series, rows, width = history.shape
    devices = lax.axis_size("tm")
    groups = lax.axis_size("series")
    assert local_series == 2 and devices % 4 == 0 and WINDOW == 2 * rows
    patches = rows * devices
    position = lax.axis_index("tm")
    quad, chip, core = position // 4, (position // 2) % 2, position % 2
    chip_swap, core_swap, near_route, far_route = routes(devices)

    def move(block, route):
        return lax.ppermute(block, "tm", route)

    def part(array, index):
        return lax.dynamic_index_in_dim(array, index, 0, keepdims=False)

    mine = part(history, chip)
    other = part(history, 1 - chip)
    away = move(other, chip_swap)
    near = move(mine, near_route)
    mine_beside = move(mine, core_swap)
    scale = (width // HEADS) ** (-0.5) * math.log2(math.e)
    place = position.astype(jnp.int32)[None]
    attention = functools.partial(attend, place, head_window, lengths, input_proj, scale)

    home_queries, *home_ready = project(mine, mine_beside, input_proj, scale)
    away, home_queries = lax.optimization_barrier((away, home_queries))
    far = move(away, far_route)
    away_beside = move(away, core_swap)
    near, home_queries = lax.optimization_barrier((near, home_queries))
    near_beside = move(near, core_swap)
    away_out, *away_ready = attention(
        False,
        [(0, [away, away_beside]), (1, [near, near_beside])],
        [(-1, home_ready)],
        keep=2,
    )
    away_out, far = lax.optimization_barrier((away_out, far))
    other_attended = move(away_out, chip_swap)
    far_beside = move(far, core_swap)
    (mine_attended,) = attention(
        True,
        [(-1, [far, far_beside])],
        [(0, home_ready), (1, away_ready)],
        queries=home_queries,
    )

    def finish(rows_in, attended):
        hidden = (
            rows_in.astype(jnp.float32)
            + jnp.dot(attended, output_proj, preferred_element_type=jnp.float32)
        ).astype(jnp.bfloat16)
        branch = jnp.dot(hidden, mixer_down, preferred_element_type=jnp.float32).astype(
            jnp.bfloat16
        )
        return hidden, branch

    own_group = lax.axis_index("series")

    def from_groups(branch):
        gathered = [branch]
        for shift in range(1, groups):
            route = [((g + shift) % groups, g) for g in range(groups)]
            gathered.append(lax.ppermute(branch, "series", route))
        return gathered

    mine_hidden, mine_branch = finish(mine, mine_attended)
    mine_branches = from_groups(mine_branch)
    other_attended, mine_attended = lax.optimization_barrier((other_attended, mine_attended))
    other_hidden, other_branch = finish(other, other_attended)
    other_branches = from_groups(other_branch)

    return mix(
        place,
        own_group.astype(jnp.int32)[None],
        series_mix.astype(jnp.float32),
        mixer_up,
        (mine_hidden, other_hidden),
        (mine_branches, other_branches),
    )


def solution(mesh):
    in_specs = (P("series", "tm", None), P("series"), P(), P(), P(), P(), P(), P())
    out_specs = P("series", "tm", None)
    return jax.shard_map(
        on_device, mesh=mesh, in_specs=in_specs, out_specs=out_specs, check_vma=False
    )
```

time: 123 us -> 84.7 us (0.69)
  Pallas kernels: 64.1 us -> 43.2 us
  matrix products: 20.4 us -> 5.43 us
  waiting for transfers between devices: 14.2 us -> 18.9 us
  other arithmetic: 4.2 us -> 0.58 us
  starting transfers between devices: 13.8 us -> 10.5 us
    pallas_call x5 -> x4, Pallas kernels: 64.1 us -> 43.2 us  [the longest x2 31.6 us: attend(): pl.pallas_call(body, out_shape=tuple(out_shape), grid_spec=pltpu.Prefetch...]
    dot_general x4 -> x0, matrix products: 15.1 us -> none  [the longest x2 8.65 us: output(): jnp.dot(combined(which), mixer_up, preferred_element_type=jnp.float32)]
    ppermute x8, starting transfers between devices: 11.7 us -> 8.43 us  [move(): return lax.ppermute(block, 'tm', route)]
    another operation x5 -> x0, other arithmetic: 3.07 us -> none  [the longest x3 1.86 us: slots(): jnp.stack([f + c for f in firsts for c in (core, 1 - core)])]
    ppermute x8, waiting for transfers between devices: 5.92 us -> 8.72 us  [move(): return lax.ppermute(block, 'tm', route)]
    unnamed x18 -> x28, local copies, waits for them, and re-layouts: 0.83 us -> 3.11 us
    ppermute x2, waiting for transfers between devices: 8.33 us -> 10.2 us  [from_groups(): gathered.append(lax.ppermute(branch, 'series', route))]
    dynamic_slice x2 -> x0, local copies, waits for them, and re-layouts: 1.25 us -> none  [part(): return lax.dynamic_index_in_dim(array, index, 0, keepdims=False)]
  transfers between devices with their start and end apart: 10 -> 10, of which waited for: 3 -> 5; matrix products, arithmetic and copies ran while one was open for 13% -> 2% of each run, Pallas kernels for 53% -> 46%
where the time goes in v2:
time: 84.7 us; the launch traced here: 84.2 us
  Pallas kernels  43.2 us (51%)
  waiting for transfers between devices  18.9 us (22%)
  starting transfers between devices  10.5 us (12%)
  matrix products  5.43 us (6%)
  local copies, waits for them, and re-layouts  5.32 us (6%)
    pallas_call x2, Pallas kernels, attend(): pl.pallas_call(body, out_shape=tuple(out_shape), grid_spec=pltpu.Prefetch...  31.6 us
    ppermute x2, waiting for transfers between devices, from_groups(): gathered.append(lax.ppermute(branch, 'series', route))  10.2 us
    ppermute x8, waiting for transfers between devices, move(): return lax.ppermute(block, 'tm', route)  8.72 us
    ppermute x8, starting transfers between devices, move(): return lax.ppermute(block, 'tm', route)  8.43 us
    pallas_call x1, Pallas kernels, project(): pl.pallas_call(body, out_shape=(jax.ShapeDtypeStruct((rows, width), jnp.b...  7.04 us
    pallas_call x1, Pallas kernels, mix(): pl.pallas_call(body, out_shape=jax.ShapeDtypeStruct((2, rows, width), jnp...  4.5 us
    dot_general x2, matrix products, finish(): jnp.dot(attended, output_proj, preferred_element_type=jnp.float32)  3.87 us
    unnamed x28, local copies, waits for them, and re-layouts  3.11 us
  transfers between devices with their start and end apart: 10, of which 5 were waited for; matrix products, arithmetic and copies ran while one was open for 2% of the time, Pallas kernels for 46%

profile of v2, /device:TPU:0, one launch (start us, length us, event | category | flops | bytes accessed | tf_op | source)
XLA Modules:
  0.0 84.2 jit_solution(16448276336216673818)
XLA Ops:
  0.0 2.2 %dynamic-slice_bitcast_fusion.1 = (bf16[256,1024]{1,0:T(8,128)(2,1)S(1)}, bf16[256,1024]{1,0:T(8,128)(2,1)}) fusion(bf16[2,256,1024]{2,1,0:T(8,128)(2,1)} %param.8, s32[]{:T(128)S(6)} %select_n.20, s32[]{:T(128)S(6)} %select_n.21), kind=kLoop, calls=%fused_computation.7 | loop fusion | bytes 2097160 | tf_op jit(solution)/shard_map/jit(dynamic_index_in_dim)/squeeze | solution.py:421
  2.2 0.5 collective-permute-start.1
  2.7 2.5 %collective-permute-start = (bf16[256,1024]{1,0:T(8,128)(2,1)}, bf16[256,1024]{1,0:T(8,128)(2,1)}, u32[]{:S(2)}, u32[]{:S(2)}) collective-permute-start(bf16[256,1024]{1,0:T(8,128)(2,1)} %get-tuple-element.32), channel_id=1, source_target_pairs={{0,4},{2,6},{4,0},{6,2},{8,12},{10,14},{12,8},{14,10},{16,20},{18,... | collective-permute-start | bytes 1572872 | tf_op jit(solution)/shard_map/ppermute | solution.py:418
  5.2 1.3 %collective-permute-start.3 = (bf16[256,1024]{1,0:T(8,128)(2,1)S(1)}, bf16[256,1024]{1,0:T(8,128)(2,1)}, u32[]{:S(2)}, u32[]{:S(2)}) collective-permute-start(bf16[256,1024]{1,0:T(8,128)(2,1)S(1)} %get-tuple-element.31.first_ref), channel_id=1, source_target_pairs={{4,12},{6,14},{8,0},{10,2},{12,20},{14,22},{16,8},{18,10},{20,28},... | collective-permute-start | bytes 1572872 | tf_op jit(solution)/shard_map/ppermute | solution.py:418
  6.5 0.0 collective-permute-done.1.beside_ref
  6.5 0.8 copy-done.8
  7.3 7.0 %project.1 = (bf16[256,1024]{1,0:T(8,128)(2,1)}, bf16[2,256,1024]{2,1,0:T(8,128)(2,1)}, bf16[2,1024,256]{2,1,0:T(8,128)(2,1)}) custom-call(bf16[256,1024]{1,0:T(8,128)(2,1)} %copy-done.4, bf16[256,1024]{1,0:T(8,128)(2,1)} %copy-done.8, bf16[1024,3072]{1,0:T(8,128)(2,1)} %refs_8_.3, bf16[1024,3072]{1,0:T(8,128)(2,1)} %refs_8_.3, bf16[1024,3072]{1,0:T(8,128)(2,1)} %refs_8_.3), custom_call_target="tpu_custom_call" | custom-call | flops 2684354560 | bytes 6291456 | tf_op jit(solution)/shard_map/project/pallas_call | solution.py:54
  14.4 3.8 %collective-permute-done.refs_0_ = bf16[256,1024]{1,0:T(8,128)(2,1)} collective-permute-done((bf16[256,1024]{1,0:T(8,128)(2,1)}, bf16[256,1024]{1,0:T(8,128)(2,1)}, u32[]{:S(2)}, u32[]{:S(2)}) %collective-permute-start) | collective-permute-done | bytes 524320 | tf_op jit(solution)/shard_map/ppermute | solution.py:418
  18.1 3.1 %collective-permute-done.3.refs_2_ = bf16[256,1024]{1,0:T(8,128)(2,1)} collective-permute-done((bf16[256,1024]{1,0:T(8,128)(2,1)S(1)}, bf16[256,1024]{1,0:T(8,128)(2,1)}, u32[]{:S(2)}, u32[]{:S(2)}) %collective-permute-start.3) | collective-permute-done | bytes 524320 | tf_op jit(solution)/shard_map/ppermute | solution.py:418
  21.3 0.5 collective-permute-start.2
  21.8 3.5 %collective-permute-start.5 = (bf16[256,1024]{1,0:T(8,128)(2,1)}, bf16[256,1024]{1,0:T(8,128)(2,1)S(1)}, u32[]{:S(2)}, u32[]{:S(2)}) collective-permute-start(bf16[256,1024]{1,0:T(8,128)(2,1)} %collective-permute-done.refs_0_), channel_id=1, source_target_pairs={{0,8},{2,10},{8,16},{10,18},{12,4},{14,6},{16,24},{18,26},{20,12},... | collective-permute-start | bytes 1572872 | tf_op jit(solution)/shard_map/ppermute | solution.py:418
  25.3 0.8 copy-done.13
  26.1 17.2 %attend.2 = (bf16[256,1024]{1,0:T(8,128)(2,1)}, bf16[2,256,1024]{2,1,0:T(8,128)(2,1)}, bf16[2,1024,256]{2,1,0:T(8,128)(2,1)}) custom-call(s32[1]{0:T(128)} %bitcast.place_ref, s32[16]{0:T(128)} %window_ref.3, s32[2]{0:T(128)} %length_ref.3, bf16[256,1024]{1,0:T(8,128)(2,1)} %collective-permute-done.refs_0_, ...), custom_call_target="tpu_custom_call" | custom-call | flops 6979321856 | bytes 9437184 | tf_op jit(solution)/shard_map/attend/pallas_call | solution.py:323
  43.3 0.0 collective-permute-done.5.refs_0_
  43.3 0.1 collective-permute-start.6
  43.4 0.1 collective-permute-start.7
  43.5 1.8 %collective-permute-done.6.refs_1_ = bf16[256,1024]{1,0:T(8,128)(2,1)S(1)} collective-permute-done((bf16[256,1024]{1,0:T(8,128)(2,1)S(1)}, bf16[256,1024]{1,0:T(8,128)(2,1)S(1)}, u32[]{:S(2)}, u32[]{:S(2)}) %collective-permute-start.6) | collective-permute-done | bytes 524320 | tf_op jit(solution)/shard_map/ppermute | solution.py:418
  45.3 0.8 copy-done.9
  46.1 14.4 %attend.3 = bf16[256,1024]{1,0:T(8,128)(2,1)} custom-call(s32[1]{0:T(128)} %bitcast.place_ref, s32[16]{0:T(128)} %window_ref.3, s32[2]{0:T(128)} %length_ref.3, bf16[256,1024]{1,0:T(8,128)(2,1)} %copy-done.7, bf16[256,1024]{1,0:T(8,128)(2,1)} %copy-done.9, bf16[2,256,1024]{2,1,0:T(8,128)(2,1)} %get-tuple-element.22.refs_4_.refs_2_, ...), custom_call_target="tpu_custom_call" | custom-call | flops 4831838208 | bytes 9437184 | tf_op jit(solution)/shard_map/attend/pallas_call | solution.py:323
  60.5 1.8 %fusion.refs_0_ = bf16[256,1024]{1,0:T(8,128)(2,1)S(1)} fusion(bf16[256,1024]{1,0:T(8,128)(2,1)} %attend.3, bf16[1024,1024]{1,0:T(8,128)(2,1)S(1)} %copy-done, bf16[256,1024]{1,0:T(8,128)(2,1)S(1)} %copy-done.5), kind=kOutput, calls=%fused_computation.2 | convolution fusion | flops 537657344 | bytes 3670016 | tf_op jit(solution)/shard_map/dot_general | solution.py:457
  62.3 0.0 copy-start.1
  62.3 2.1 %fusion.1.refs_1_ = bf16[256,1024]{1,0:T(8,128)(2,1)S(1)} fusion(bf16[256,1024]{1,0:T(8,128)(2,1)} %collective-permute-done.7, bf16[1024,1024]{1,0:T(8,128)(2,1)S(1)} %copy-done, bf16[256,1024]{1,0:T(8,128)(2,1)} %get-tuple-element.32), kind=kOutput, calls=%fused_computation.3 | convolution fusion | flops 537657344 | bytes 3670016 | tf_op jit(solution)/shard_map/dot_general | solution.py:457
  64.5 0.0 copy-start.12
  64.5 0.4 convolution_convert_fusion.refs_4_
  64.9 1.6 %collective-permute-start.9 = (bf16[256,512]{1,0:T(8,128)(2,1)S(1)}, bf16[256,512]{1,0:T(8,128)(2,1)S(1)}, u32[]{:S(2)}, u32[]{:S(2)}) collective-permute-start(bf16[256,512]{1,0:T(8,128)(2,1)S(1)} %convolution_convert_fusion.refs_4_), channel_id=1, source_target_pairs={{1,0},{0,1},{3,2},{2,3},{5,4},{4,5},{7,6},{6,7},{9,8},{8,9},{11,10... | collective-permute-start | bytes 786440 | tf_op jit(solution)/shard_map/ppermute | solution.py:470
  66.5 1.1 %convolution_convert_fusion.1.refs_2_ = bf16[256,512]{1,0:T(8,128)(2,1)} fusion(bf16[256,1024]{1,0:T(8,128)(2,1)S(1)} %fusion.refs_0_, bf16[1024,512]{1,0:T(8,128)(2,1)S(1)} %copy-done.1), kind=kOutput, calls=%fused_computation.5 | convolution fusion | flops 268566528 | bytes 1835008 | tf_op jit(solution)/shard_map/dot_general | solution.py:459
  67.6 0.5 collective-permute-start.8
  68.2 0.6 convert_element_type.21.mix_ref
  68.7 5.4 %collective-permute-done.9.refs_5_ = bf16[256,512]{1,0:T(8,128)(2,1)S(1)} collective-permute-done((bf16[256,512]{1,0:T(8,128)(2,1)S(1)}, bf16[256,512]{1,0:T(8,128)(2,1)S(1)}, u32[]{:S(2)}, u32[]{:S(2)}) %collective-permute-start.9) | collective-permute-done | bytes 262176 | tf_op jit(solution)/shard_map/ppermute | solution.py:470
  74.2 4.8 %collective-permute-done.8.refs_3_ = bf16[256,512]{1,0:T(8,128)(2,1)S(1)} collective-permute-done((bf16[256,512]{1,0:T(8,128)(2,1)}, bf16[256,512]{1,0:T(8,128)(2,1)S(1)}, u32[]{:S(2)}, u32[]{:S(2)}) %collective-permute-start.8) | collective-permute-done | bytes 262176 | tf_op jit(solution)/shard_map/ppermute | solution.py:470
  79.0 0.7 copy-done.11
  79.7 4.5 %mix.1 = bf16[2,256,1024]{2,1,0:T(8,128)(2,1)} custom-call(s32[1]{0:T(128)} %bitcast.place_ref, s32[1]{0:T(128)} %bitcast.1.group_ref, f32[4,4]{1,0:T(4,128)} %convert_element_type.21.mix_ref, bf16[512,1024]{1,0:T(8,128)(2,1)} %weight_ref.1, bf16[256,1024]{1,0:T(8,128)(2,1)} %copy-done.2, bf16[256,1024]{1,0:T(8,128)(2,1)} %copy-done.3, ...), custom_call_target="tpu_custom_call" | custom-call | flops 536870912 | bytes 1048576 | tf_op jit(solution)/shard_map/mix/pallas_call | solution.py:387
  (26 shorter events, 0.1 us)
Async XLA Ops:
  0.0 60.5 %copy-start = (bf16[1024,1024]{1,0:T(8,128)(2,1)S(1)}, bf16[1024,1024]{1,0:T(8,128)(2,1)}, u32[]{:S(2)}) copy-start(bf16[1024,1024]{1,0:T(8,128)(2,1)} %param.12) | copy-start | bytes 6291460
  2.2 4.3 %copy-start.4 = (bf16[256,1024]{1,0:T(8,128)(2,1)}, bf16[256,1024]{1,0:T(8,128)(2,1)S(1)}, u32[]{:S(2)}) copy-start(bf16[256,1024]{1,0:T(8,128)(2,1)S(1)} %get-tuple-element.31.first_ref) | copy-start | bytes 1572868
  2.2 4.3 %collective-permute-start.1 = (bf16[256,1024]{1,0:T(8,128)(2,1)S(1)}, bf16[256,1024]{1,0:T(8,128)(2,1)S(1)}, u32[]{:S(2)}, u32[]{:S(2)}) collective-permute-start(bf16[256,1024]{1,0:T(8,128)(2,1)S(1)} %get-tuple-element.31.first_ref), channel_id=1, source_target_pairs={{0,2},{2,0},{4,6},{6,4},{8,10},{10,8},{12,14},{14,12},{16,18},{18,... | collective-permute-start | bytes 1572872 | tf_op jit(solution)/shard_map/ppermute | solution.py:418
  2.7 15.4 %collective-permute-start = (bf16[256,1024]{1,0:T(8,128)(2,1)}, bf16[256,1024]{1,0:T(8,128)(2,1)}, u32[]{:S(2)}, u32[]{:S(2)}) collective-permute-start(bf16[256,1024]{1,0:T(8,128)(2,1)} %get-tuple-element.32), channel_id=1, source_target_pairs={{0,4},{2,6},{4,0},{6,2},{8,12},{10,14},{12,8},{14,10},{16,20},{18,... | collective-permute-start | bytes 1572872 | tf_op jit(solution)/shard_map/ppermute | solution.py:418
  5.2 16.0 %collective-permute-start.3 = (bf16[256,1024]{1,0:T(8,128)(2,1)S(1)}, bf16[256,1024]{1,0:T(8,128)(2,1)}, u32[]{:S(2)}, u32[]{:S(2)}) collective-permute-start(bf16[256,1024]{1,0:T(8,128)(2,1)S(1)} %get-tuple-element.31.first_ref), channel_id=1, source_target_pairs={{4,12},{6,14},{8,0},{10,2},{12,20},{14,22},{16,8},{18,10},{20,28},... | collective-permute-start | bytes 1572872 | tf_op jit(solution)/shard_map/ppermute | solution.py:418
  6.5 0.8 copy-start.8
  21.3 4.0 %collective-permute-start.4 = (bf16[256,1024]{1,0:T(8,128)(2,1)}, bf16[256,1024]{1,0:T(8,128)(2,1)S(1)}, u32[]{:S(2)}, u32[]{:S(2)}) collective-permute-start(bf16[256,1024]{1,0:T(8,128)(2,1)} %collective-permute-done.3.refs_2_), channel_id=1, source_target_pairs={{0,2},{2,0},{4,6},{6,4},{8,10},{10,8},{12,14},{14,12},{16,18},{18,... | collective-permute-start | bytes 1572872 | tf_op jit(solution)/shard_map/ppermute | solution.py:418
  21.3 4.0 %collective-permute-start.2 = (bf16[256,1024]{1,0:T(8,128)(2,1)}, bf16[256,1024]{1,0:T(8,128)(2,1)}, u32[]{:S(2)}, u32[]{:S(2)}) collective-permute-start(bf16[256,1024]{1,0:T(8,128)(2,1)} %collective-permute-done.refs_0_), channel_id=1, source_target_pairs={{0,2},{2,0},{4,6},{6,4},{8,10},{10,8},{12,14},{14,12},{16,18},{18,... | collective-permute-start | bytes 1572872 | tf_op jit(solution)/shard_map/ppermute | solution.py:418
  21.8 21.5 %collective-permute-start.5 = (bf16[256,1024]{1,0:T(8,128)(2,1)}, bf16[256,1024]{1,0:T(8,128)(2,1)S(1)}, u32[]{:S(2)}, u32[]{:S(2)}) collective-permute-start(bf16[256,1024]{1,0:T(8,128)(2,1)} %collective-permute-done.refs_0_), channel_id=1, source_target_pairs={{0,8},{2,10},{8,16},{10,18},{12,4},{14,6},{16,24},{18,26},{20,12},... | collective-permute-start | bytes 1572872 | tf_op jit(solution)/shard_map/ppermute | solution.py:418
  25.3 0.8 copy-start.13
  43.3 2.8 %copy-start.7 = (bf16[256,1024]{1,0:T(8,128)(2,1)}, bf16[256,1024]{1,0:T(8,128)(2,1)S(1)}, u32[]{:S(2)}) copy-start(bf16[256,1024]{1,0:T(8,128)(2,1)S(1)} %collective-permute-done.5.refs_0_) | copy-start | bytes 1572868
  43.3 2.0 %collective-permute-start.6 = (bf16[256,1024]{1,0:T(8,128)(2,1)S(1)}, bf16[256,1024]{1,0:T(8,128)(2,1)S(1)}, u32[]{:S(2)}, u32[]{:S(2)}) collective-permute-start(bf16[256,1024]{1,0:T(8,128)(2,1)S(1)} %collective-permute-done.5.refs_0_), channel_id=1, source_target_pairs={{0,2},{2,0},{4,6},{6,4},{8,10},{10,8},{12,14},{14,12},{16,18},{18,... | collective-permute-start | bytes 1572872 | tf_op jit(solution)/shard_map/ppermute | solution.py:418
  43.4 17.1 %collective-permute-start.7 = (bf16[256,1024]{1,0:T(8,128)(2,1)}, bf16[256,1024]{1,0:T(8,128)(2,1)}, u32[]{:S(2)}, u32[]{:S(2)}) collective-permute-start(bf16[256,1024]{1,0:T(8,128)(2,1)} %get-tuple-element.29), channel_id=1, source_target_pairs={{0,4},{2,6},{4,0},{6,2},{8,12},{10,14},{12,8},{14,10},{16,20},{18,... | collective-permute-start | bytes 1572872 | tf_op jit(solution)/shard_map/ppermute | solution.py:418
  45.3 0.8 copy-start.9
  46.1 14.4 %copy-start.5 = (bf16[256,1024]{1,0:T(8,128)(2,1)S(1)}, bf16[256,1024]{1,0:T(8,128)(2,1)}, u32[]{:S(2)}) copy-start(bf16[256,1024]{1,0:T(8,128)(2,1)} %copy-done.4) | copy-start | bytes 1572868
  62.3 4.2 %copy-start.2 = (bf16[256,1024]{1,0:T(8,128)(2,1)}, bf16[256,1024]{1,0:T(8,128)(2,1)S(1)}, u32[]{:S(2)}) copy-start(bf16[256,1024]{1,0:T(8,128)(2,1)S(1)} %fusion.refs_0_) | copy-start | bytes 1572868
  62.3 2.1 %copy-start.1 = (bf16[1024,512]{1,0:T(8,128)(2,1)S(1)}, bf16[1024,512]{1,0:T(8,128)(2,1)}, u32[]{:S(2)}) copy-start(bf16[1024,512]{1,0:T(8,128)(2,1)} %param.13) | copy-start | bytes 3145732
  64.5 14.5 %copy-start.3 = (bf16[256,1024]{1,0:T(8,128)(2,1)}, bf16[256,1024]{1,0:T(8,128)(2,1)S(1)}, u32[]{:S(2)}) copy-start(bf16[256,1024]{1,0:T(8,128)(2,1)S(1)} %fusion.1.refs_1_) | copy-start | bytes 1572868
  64.5 3.7 %copy-start.12 = (bf16[4,4]{1,0:T(4,128)(2,1)S(1)}, bf16[4,4]{1,0:T(4,128)(2,1)}, u32[]{:S(2)}) copy-start(bf16[4,4]{1,0:T(4,128)(2,1)} %param.15) | copy-start | bytes 100
  64.9 14.0 %copy-start.6 = (bf16[256,512]{1,0:T(8,128)(2,1)}, bf16[256,512]{1,0:T(8,128)(2,1)S(1)}, u32[]{:S(2)}) copy-start(bf16[256,512]{1,0:T(8,128)(2,1)S(1)} %convolution_convert_fusion.refs_4_) | copy-start | bytes 786436
  64.9 9.2 %collective-permute-start.9 = (bf16[256,512]{1,0:T(8,128)(2,1)S(1)}, bf16[256,512]{1,0:T(8,128)(2,1)S(1)}, u32[]{:S(2)}, u32[]{:S(2)}) collective-permute-start(bf16[256,512]{1,0:T(8,128)(2,1)S(1)} %convolution_convert_fusion.refs_4_), channel_id=1, source_target_pairs={{1,0},{0,1},{3,2},{2,3},{5,4},{4,5},{7,6},{6,7},{9,8},{8,9},{11,10... | collective-permute-start | bytes 786440 | tf_op jit(solution)/shard_map/ppermute | solution.py:470
  67.6 11.3 %collective-permute-start.8 = (bf16[256,512]{1,0:T(8,128)(2,1)}, bf16[256,512]{1,0:T(8,128)(2,1)S(1)}, u32[]{:S(2)}, u32[]{:S(2)}) collective-permute-start(bf16[256,512]{1,0:T(8,128)(2,1)} %convolution_convert_fusion.1.refs_2_), channel_id=1, source_target_pairs={{1,0},{0,1},{3,2},{2,3},{5,4},{4,5},{7,6},{6,7},{9,8},{8,9},{11,10... | collective-permute-start | bytes 786440 | tf_op jit(solution)/shard_map/ppermute | solution.py:470
  74.2 4.8 %copy-start.10 = (bf16[256,512]{1,0:T(8,128)(2,1)}, bf16[256,512]{1,0:T(8,128)(2,1)S(1)}, u32[]{:S(2)}) copy-start(bf16[256,512]{1,0:T(8,128)(2,1)S(1)} %collective-permute-done.9.refs_5_) | copy-start | bytes 786436
  79.0 0.7 copy-start.11

commit v3 on v2

--- a/solution.py
+++ b/solution.py
@@ -72,7 +72,10 @@
     )(first, beside, weight, weight, weight)
 
 
-def attend(place, head_window, lengths, weight, scale, home, raw, ready, queries=None, keep=0):
+def attend(
+    place, head_window, lengths, weight, output_proj, mixer_down, scale, home, raw, ready,
+    own=None, keep=0,
+):
     raw_sides = [side for side, _ in raw]
     ready_sides = [side for side, _ in ready]
     raw = [block for _, blocks in raw for block in blocks]
@@ -100,12 +103,14 @@
         take = lambda count: [refs.pop(0) for _ in range(count)]
         raw_refs = take(raw_count)
         ready_refs = take(2 * ready_count)
-        query_ref = take(1)[0] if queries is not None else None
-        wq_ref = take(1)[0] if queries is None else None
-        wk_ref, wv_ref, out_ref = take(3)
+        rows_ref, query_ref = take(2) if home else (raw_refs[0], None)
+        wq_ref = None if home else take(1)[0]
+        wk_ref, wv_ref, wo_hbm, down_hbm = take(4)
+        hidden_ref, branch_ref = take(2)
         keep_refs = take(2) if keep else None
         key_scr, weight_scr, row_scr, query_scr = take(4)
         value_scrs, score_scrs, top_scrs = take(2), take(2), take(2)
+        attended_scr, wo_scr, down_scr, copy_sems = take(4)
         index = pl.program_id(0)
         position = place_ref[0]
         core = position % 2
@@ -119,8 +124,15 @@
             offset = core if not beside else 1 - core
             return 2 + 2 * side * (1 - 2 * chip) + offset
 
+        copies = [
+            pltpu.make_async_copy(wo_hbm, wo_scr, copy_sems.at[0]),
+            pltpu.make_async_copy(down_hbm, down_scr, copy_sems.at[1]),
+        ]
+
         @pl.when(index == 0)
         def _():
+            for copy in copies:
+                copy.start()
             row_scr[...] = lax.broadcasted_iota(jnp.int32, (rows, LANES), 0)
 
         def front(parity, value_scr, score_scr, top_scr):
@@ -257,7 +269,8 @@
                     total = sums[head][head_size : head_size + 1]
                     factor = jnp.where(query_valid, 1.0 / total, 0.0)
                     outs.append(sums[head][:head_size] * factor)
-                out_ref[...] = jnp.concatenate(outs, 0).T.astype(out_ref.dtype)
+                where = pl.ds(pl.multiple_of(jnp.maximum(index - 1, 0) * LANES, LANES), LANES)
+                attended_scr[:, where] = jnp.concatenate(outs, 0).T.astype(jnp.bfloat16)
 
             units = [
                 functools.partial(add_block, step, head)
@@ -288,6 +301,14 @@
         def _():
             for unit in back(*sets[(pairs - 1) % 2]):
                 unit()
+            for copy in copies:
+                copy.wait()
+            update = jnp.dot(attended_scr[...], wo_scr[...], preferred_element_type=jnp.float32)
+            hidden = (rows_ref[...].astype(jnp.float32) + update).astype(jnp.bfloat16)
+            hidden_ref[...] = hidden
+            branch_ref[...] = jnp.dot(
+                hidden, down_scr[...], preferred_element_type=jnp.float32
+            ).astype(jnp.bfloat16)
 
     ahead = lambda g: jnp.minimum(g, pairs - 1)
     block = pl.BlockSpec((rows, LANES), lambda g, *_: (0, ahead(g)))
@@ -301,18 +322,23 @@
     for keys, values in ready:
         in_specs += [key_spec(2), value_spec(2)]
         operands += [keys, values]
-    if queries is not None:
-        in_specs.append(block)
-        operands.append(queries)
+    whole = lambda shape: pl.BlockSpec(shape, lambda g, *_: (0, 0))
+    if home:
+        in_specs += [whole((rows, width)), block]
+        operands += own
     else:
         in_specs.append(
             pl.BlockSpec((width, 2 * LANES), lambda g, *_: (0, ahead(g) // 2))
         )
         operands.append(weight)
-    in_specs += [weight_spec(1), weight_spec(2)]
-    operands += [weight, weight]
-    out_shape = [jax.ShapeDtypeStruct((rows, width), jnp.bfloat16)]
-    out_specs = [pl.BlockSpec((rows, LANES), lambda g, *_: (0, jnp.maximum(g - 1, 0)))]
+    in_specs += [weight_spec(1), weight_spec(2)] + [pl.BlockSpec(memory_space=pl.ANY)] * 2
+    operands += [weight, weight, output_proj, mixer_down]
+    inner = mixer_down.shape[1]
+    out_shape = [
+        jax.ShapeDtypeStruct((rows, width), jnp.bfloat16),
+        jax.ShapeDtypeStruct((rows, inner), jnp.bfloat16),
+    ]
+    out_specs = [whole((rows, width)), whole((rows, inner))]
     if keep:
         out_shape += [
             jax.ShapeDtypeStruct((keep, rows, width), jnp.bfloat16),
@@ -336,7 +362,13 @@
             ]
             + twice((slot_count, LANES, rows), jnp.bfloat16)
             + twice((2, steps, rows, cols), jnp.float32)
-            + twice((2, 1, cols), jnp.float32),
+            + twice((2, 1, cols), jnp.float32)
+            + [
+                pltpu.VMEM((rows, width), jnp.bfloat16),
+                pltpu.VMEM(output_proj.shape, jnp.bfloat16),
+                pltpu.VMEM(mixer_down.shape, jnp.bfloat16),
+                pltpu.SemaphoreType.DMA((2,)),
+            ],
         ),
         cost_estimate=pl.CostEstimate(
             flops=(8 * steps * rows + 4 * raw_count * width) * rows * width,
@@ -427,7 +459,9 @@
     mine_beside = move(mine, core_swap)
     scale = (width // HEADS) ** (-0.5) * math.log2(math.e)
     place = position.astype(jnp.int32)[None]
-    attention = functools.partial(attend, place, head_window, lengths, input_proj, scale)
+    attention = functools.partial(
+        attend, place, head_window, lengths, input_proj, output_proj, mixer_down, scale
+    )
 
     home_queries, *home_ready = project(mine, mine_beside, input_proj, scale)
     away, home_queries = lax.optimization_barrier((away, home_queries))
@@ -435,47 +469,42 @@
     away_beside = move(away, core_swap)
     near, home_queries = lax.optimization_barrier((near, home_queries))
     near_beside = move(near, core_swap)
-    away_out, *away_ready = attention(
+    away_hidden, away_branch, *away_ready = attention(
         False,
         [(0, [away, away_beside]), (1, [near, near_beside])],
         [(-1, home_ready)],
         keep=2,
     )
-    away_out, far = lax.optimization_barrier((away_out, far))
-    other_attended = move(away_out, chip_swap)
+    away_hidden, far = lax.optimization_barrier((away_hidden, far))
     far_beside = move(far, core_swap)
-    (mine_attended,) = attention(
+
+    def down(hidden):
+        return jnp.dot(hidden, mixer_down, preferred_element_type=jnp.float32).astype(jnp.bfloat16)
+
+    other_hidden = move(away_hidden, chip_swap)
+    other_branches = []
+    for shift in range(1, groups):
+        route = [
+            (i * groups + (g + shift) % groups, home * groups + g)
+            for g in range(groups)
+            for i, home in chip_swap
+        ]
+        other_branches.append(lax.ppermute(away_branch, ("tm", "series"), route))
+
+    mine_hidden, mine_branch = attention(
         True,
         [(-1, [far, far_beside])],
         [(0, home_ready), (1, away_ready)],
-        queries=home_queries,
+        own=[mine, home_queries],
     )
-
-    def finish(rows_in, attended):
-        hidden = (
-            rows_in.astype(jnp.float32)
-            + jnp.dot(attended, output_proj, preferred_element_type=jnp.float32)
-        ).astype(jnp.bfloat16)
-        branch = jnp.dot(hidden, mixer_down, preferred_element_type=jnp.float32).astype(
-            jnp.bfloat16
-        )
-        return hidden, branch
+    mine_branches = [mine_branch]
+    for shift in range(1, groups):
+        route = [((g + shift) % groups, g) for g in range(groups)]
+        mine_branches.append(lax.ppermute(mine_branch, "series", route))
+    other_hidden, mine_branch = lax.optimization_barrier((other_hidden, mine_branch))
+    other_branches = [down(other_hidden)] + other_branches
 
     own_group = lax.axis_index("series")
-
-    def from_groups(branch):
-        gathered = [branch]
-        for shift in range(1, groups):
-            route = [((g + shift) % groups, g) for g in range(groups)]
-            gathered.append(lax.ppermute(branch, "series", route))
-        return gathered
-
-    mine_hidden, mine_branch = finish(mine, mine_attended)
-    mine_branches = from_groups(mine_branch)
-    other_attended, mine_attended = lax.optimization_barrier((other_attended, mine_attended))
-    other_hidden, other_branch = finish(other, other_attended)
-    other_branches = from_groups(other_branch)
-
     return mix(
         place,
         own_group.astype(jnp.int32)[None],

time: 84.7 us -> 78.1 us (0.922)
  waiting for transfers between devices: 18.9 us -> 13.3 us
  matrix products: 5.43 us -> 1.13 us
  Pallas kernels: 43.2 us -> 45.8 us
  starting transfers between devices: 10.5 us -> 12.1 us
    dot_general x4 -> x1, matrix products: 5.43 us -> 1.13 us  [down(): jnp.dot(hidden, mixer_down, preferred_element_type=jnp.float32)]
    ppermute x2, waiting for transfers between devices: 10.2 us -> 6.62 us  [the longest x1 6.61 us: on_device(): mine_branches.append(lax.ppermute(mine_branch, 'series', route))]
    pallas_call x2, Pallas kernels: 31.6 us -> 34.3 us  [attend(): pl.pallas_call(body, out_shape=tuple(out_shape), grid_spec=pltpu.Prefetch...]
    ppermute x8, waiting for transfers between devices: 8.72 us -> 6.71 us  [move(): return lax.ppermute(block, 'tm', route)]
    ppermute x2, starting transfers between devices: 2.09 us -> 3.54 us  [the longest x1 2.94 us: on_device(): other_branches.append(lax.ppermute(away_branch, ('tm', 'series'), route))]
    squeeze x1, local copies, waits for them, and re-layouts: 2.22 us -> 1.27 us  [part(): return lax.dynamic_index_in_dim(array, index, 0, keepdims=False)]
    unnamed x28 -> x26, local copies, waits for them, and re-layouts: 3.11 us -> 3.27 us
  transfers between devices with their start and end apart: 10 -> 10, of which waited for: 5 -> 3; matrix products, arithmetic and copies ran while one was open for 2% -> 2% of each run, Pallas kernels for 46% -> 53%
where the time goes in v3:
time: 78.1 us; the launch traced here: 77.7 us
  Pallas kernels  45.8 us (59%)
  waiting for transfers between devices  13.3 us (17%)
  starting transfers between devices  12.1 us (15%)
  local copies, waits for them, and re-layouts  4.53 us (6%)
  matrix products  1.13 us (1%)
    pallas_call x2, Pallas kernels, attend(): pl.pallas_call(body, out_shape=tuple(out_shape), grid_spec=pltpu.Prefetch...  34.3 us
    ppermute x8, starting transfers between devices, move(): return lax.ppermute(block, 'tm', route)  8.57 us
    pallas_call x1, Pallas kernels, project(): pl.pallas_call(body, out_shape=(jax.ShapeDtypeStruct((rows, width), jnp.b...  7.04 us
    ppermute x8, waiting for transfers between devices, move(): return lax.ppermute(block, 'tm', route)  6.71 us
    ppermute x1, waiting for transfers between devices, on_device(): mine_branches.append(lax.ppermute(mine_branch, 'series', route))  6.61 us
    pallas_call x1, Pallas kernels, mix(): pl.pallas_call(body, out_shape=jax.ShapeDtypeStruct((2, rows, width), jnp...  4.5 us
    unnamed x26, local copies, waits for them, and re-layouts  3.27 us
    ppermute x1, starting transfers between devices, on_device(): other_branches.append(lax.ppermute(away_branch, ('tm', 'series'), route))  2.94 us
  transfers between devices with their start and end apart: 10, of which 3 were waited for; matrix products, arithmetic and copies ran while one was open for 2% of the time, Pallas kernels for 53%

profile of v3, /device:TPU:0, one launch (start us, length us, event | category | flops | bytes accessed | tf_op | source)
XLA Modules:
  0.0 77.7 jit_solution(10298760379997697620)
XLA Ops:
  0.0 1.3 %dynamic-slice_bitcast_fusion = (bf16[256,1024]{1,0:T(8,128)(2,1)S(1)}, bf16[256,1024]{1,0:T(8,128)(2,1)S(1)}) fusion(bf16[2,256,1024]{2,1,0:T(8,128)(2,1)} %param.8, s32[]{:T(128)S(6)} %select_n.21, s32[]{:T(128)S(6)} %select_n.20), kind=kLoop, calls=%fused_computation.1 | loop fusion | bytes 2097160 | tf_op jit(solution)/shard_map/jit(dynamic_index_in_dim)/squeeze | solution.py:453
  1.3 0.6 collective-permute-start.1
  1.8 2.6 %collective-permute-start = (bf16[256,1024]{1,0:T(8,128)(2,1)S(1)}, bf16[256,1024]{1,0:T(8,128)(2,1)S(1)}, u32[]{:S(2)}, u32[]{:S(2)}) collective-permute-start(bf16[256,1024]{1,0:T(8,128)(2,1)S(1)} %get-tuple-element.38), channel_id=1, source_target_pairs={{0,4},{2,6},{4,0},{6,2},{8,12},{10,14},{12,8},{14,10},{16,20},{18,... | collective-permute-start | bytes 1572872 | tf_op jit(solution)/shard_map/ppermute | solution.py:450
  4.4 1.3 %collective-permute-start.3 = (bf16[256,1024]{1,0:T(8,128)(2,1)S(1)}, bf16[256,1024]{1,0:T(8,128)(2,1)S(1)}, u32[]{:S(2)}, u32[]{:S(2)}) collective-permute-start(bf16[256,1024]{1,0:T(8,128)(2,1)S(1)} %get-tuple-element.37.first_ref.refs_6_), channel_id=1, source_target_pairs={{4,12},{6,14},{8,0},{10,2},{12,20},{14,22},{16,8},{18,10},{20,28},... | collective-permute-start | bytes 1572872 | tf_op jit(solution)/shard_map/ppermute | solution.py:450
  5.7 0.0 collective-permute-done.1.beside_ref
  5.7 0.8 %copy-done.9 = bf16[256,1024]{1,0:T(8,128)(2,1)} copy-done((bf16[256,1024]{1,0:T(8,128)(2,1)}, bf16[256,1024]{1,0:T(8,128)(2,1)S(1)}, u32[]{:S(2)}) %copy-start.9) | copy-done | bytes 524312
  6.6 7.0 %project.1 = (bf16[256,1024]{1,0:T(8,128)(2,1)}, bf16[2,256,1024]{2,1,0:T(8,128)(2,1)}, bf16[2,1024,256]{2,1,0:T(8,128)(2,1)}) custom-call(bf16[256,1024]{1,0:T(8,128)(2,1)} %copy-done.1, bf16[256,1024]{1,0:T(8,128)(2,1)} %copy-done.9, bf16[1024,3072]{1,0:T(8,128)(2,1)} %refs_9_.3, bf16[1024,3072]{1,0:T(8,128)(2,1)} %refs_9_.3, bf16[1024,3072]{1,0:T(8,128)(2,1)} %refs_9_.3), custom_call_target="tpu_custom_call" | custom-call | flops 2684354560 | bytes 6291456 | tf_op jit(solution)/shard_map/project/pallas_call | solution.py:54
  13.6 3.4 %collective-permute-done.refs_0_ = bf16[256,1024]{1,0:T(8,128)(2,1)S(1)} collective-permute-done((bf16[256,1024]{1,0:T(8,128)(2,1)S(1)}, bf16[256,1024]{1,0:T(8,128)(2,1)S(1)}, u32[]{:S(2)}, u32[]{:S(2)}) %collective-permute-start) | collective-permute-done | bytes 524320 | tf_op jit(solution)/shard_map/ppermute | solution.py:450
  16.9 3.3 %collective-permute-done.3.refs_2_ = bf16[256,1024]{1,0:T(8,128)(2,1)S(1)} collective-permute-done((bf16[256,1024]{1,0:T(8,128)(2,1)S(1)}, bf16[256,1024]{1,0:T(8,128)(2,1)S(1)}, u32[]{:S(2)}, u32[]{:S(2)}) %collective-permute-start.3) | collective-permute-done | bytes 524320 | tf_op jit(solution)/shard_map/ppermute | solution.py:450
  20.3 0.0 collective-permute-start.4
  20.3 0.5 collective-permute-start.2
  20.8 3.5 %collective-permute-start.5 = (bf16[256,1024]{1,0:T(8,128)(2,1)S(1)}, bf16[256,1024]{1,0:T(8,128)(2,1)S(1)}, u32[]{:S(2)}, u32[]{:S(2)}) collective-permute-start(bf16[256,1024]{1,0:T(8,128)(2,1)S(1)} %collective-permute-done.refs_0_), channel_id=1, source_target_pairs={{0,8},{2,10},{8,16},{10,18},{12,4},{14,6},{16,24},{18,26},{20,12},... | collective-permute-start | bytes 1572872 | tf_op jit(solution)/shard_map/ppermute | solution.py:450
  24.3 0.0 collective-permute-done.4.refs_3_
  24.3 0.0 collective-permute-done.2.refs_1_
  24.4 0.8 copy-done.7
  25.1 0.2 copy-done.8
  25.3 18.6 %attend.2 = (bf16[256,1024]{1,0:T(8,128)(2,1)}, bf16[256,512]{1,0:T(8,128)(2,1)}, bf16[2,256,1024]{2,1,0:T(8,128)(2,1)}, bf16[2,1024,256]{2,1,0:T(8,128)(2,1)}) custom-call(s32[1]{0:T(128)} %bitcast.place_ref, s32[16]{0:T(128)} %window_ref.3, s32[2]{0:T(128)} %length_ref.3, bf16[256,1024]{1,0:T(8,128)(2,1)} %copy-done.4, bf16[256,1024]{1,0:T(8,128)(2,1)} %copy-done.8, ...), custom_call_target="tpu_custom_call" | custom-call | flops 6979321856 | bytes 9437184 | tf_op jit(solution)/shard_map/attend/pallas_call | solution.py:349
  43.9 0.0 collective-permute-done.5.refs_0_
  43.9 0.1 collective-permute-start.6
  44.0 0.1 collective-permute-start.7
  44.1 0.6 convert_element_type.6.mix_ref
  44.7 2.9 %collective-permute-start.9 = (bf16[256,512]{1,0:T(8,128)(2,1)}, bf16[256,512]{1,0:T(8,128)(2,1)S(1)}, u32[]{:S(2)}, u32[]{:S(2)}) collective-permute-start(bf16[256,512]{1,0:T(8,128)(2,1)} %get-tuple-element.36), channel_id=1, source_target_pairs={{1,4},{3,6},{5,0},{7,2},{9,12},{11,14},{13,8},{15,10},{17,20},{19,... | collective-permute-start | bytes 786440 | tf_op jit(solution)/shard_map/ppermute | solution.py:492
  47.6 0.0 collective-permute-done.6.refs_1_
  47.6 0.8 %copy-done.6 = bf16[256,1024]{1,0:T(8,128)(2,1)} copy-done((bf16[256,1024]{1,0:T(8,128)(2,1)}, bf16[256,1024]{1,0:T(8,128)(2,1)S(1)}, u32[]{:S(2)}) %copy-start.6) | copy-done | bytes 524312
  48.4 15.7 %attend.3 = (bf16[256,1024]{1,0:T(8,128)(2,1)}, bf16[256,512]{1,0:T(8,128)(2,1)}) custom-call(s32[1]{0:T(128)} %bitcast.place_ref, s32[16]{0:T(128)} %window_ref.3, s32[2]{0:T(128)} %length_ref.3, bf16[256,1024]{1,0:T(8,128)(2,1)} %copy-done.3, bf16[256,1024]{1,0:T(8,128)(2,1)} %copy-done.6, bf16[2,256,1024]{2,1,0:T(8,128)(2,1)} %get-tuple-element.25.refs_4_.refs_2_, ...), custom_call_target="tpu_custom_call" | custom-call | flops 4831838208 | bytes 9437184 | tf_op jit(solution)/shard_map/attend/pallas_call | solution.py:349
  64.1 0.6 collective-permute-start.8
  64.7 0.0 collective-permute-done.7.refs_1_
  64.7 1.1 %convolution_convert_fusion.refs_4_ = bf16[256,512]{1,0:T(8,128)(2,1)} fusion(bf16[256,1024]{1,0:T(8,128)(2,1)S(1)} %collective-permute-done.7.refs_1_, bf16[1024,512]{1,0:T(8,128)(2,1)S(1)} %copy-done), kind=kOutput, calls=%fused_computation | convolution fusion | flops 268566528 | bytes 1835008 | tf_op jit(solution)/shard_map/dot_general | solution.py:482
  65.8 0.0 collective-permute-done.9.refs_5_
  65.9 6.6 %collective-permute-done.8.refs_3_ = bf16[256,512]{1,0:T(8,128)(2,1)S(1)} collective-permute-done((bf16[256,512]{1,0:T(8,128)(2,1)}, bf16[256,512]{1,0:T(8,128)(2,1)S(1)}, u32[]{:S(2)}, u32[]{:S(2)}) %collective-permute-start.8) | collective-permute-done | bytes 262176 | tf_op jit(solution)/shard_map/ppermute | solution.py:503
  72.5 0.7 copy-done.11
  73.2 4.5 %mix.1 = bf16[2,256,1024]{2,1,0:T(8,128)(2,1)} custom-call(s32[1]{0:T(128)} %bitcast.place_ref, s32[1]{0:T(128)} %bitcast.1.group_ref, f32[4,4]{1,0:T(4,128)} %convert_element_type.6.mix_ref, bf16[512,1024]{1,0:T(8,128)(2,1)} %weight_ref.1, bf16[256,1024]{1,0:T(8,128)(2,1)} %get-tuple-element.32.refs_0_, bf16[256,1024]{1,0:T(8,128)(2,1)} %copy-done.2, ...), custom_call_target="tpu_custom_call" | custom-call | flops 536870912 | bytes 1048576 | tf_op jit(solution)/shard_map/mix/pallas_call | solution.py:419
  (21 shorter events, 0.0 us)
Async XLA Ops:
  1.3 4.5 %copy-start.1 = (bf16[256,1024]{1,0:T(8,128)(2,1)}, bf16[256,1024]{1,0:T(8,128)(2,1)S(1)}, u32[]{:S(2)}) copy-start(bf16[256,1024]{1,0:T(8,128)(2,1)S(1)} %get-tuple-element.37.first_ref.refs_6_) | copy-start | bytes 1572868
  1.3 4.4 %collective-permute-start.1 = (bf16[256,1024]{1,0:T(8,128)(2,1)S(1)}, bf16[256,1024]{1,0:T(8,128)(2,1)S(1)}, u32[]{:S(2)}, u32[]{:S(2)}) collective-permute-start(bf16[256,1024]{1,0:T(8,128)(2,1)S(1)} %get-tuple-element.37.first_ref.refs_6_), channel_id=1, source_target_pairs={{0,2},{2,0},{4,6},{6,4},{8,10},{10,8},{12,14},{14,12},{16,18},{18,... | collective-permute-start | bytes 1572872 | tf_op jit(solution)/shard_map/ppermute | solution.py:450
  1.8 15.1 %collective-permute-start = (bf16[256,1024]{1,0:T(8,128)(2,1)S(1)}, bf16[256,1024]{1,0:T(8,128)(2,1)S(1)}, u32[]{:S(2)}, u32[]{:S(2)}) collective-permute-start(bf16[256,1024]{1,0:T(8,128)(2,1)S(1)} %get-tuple-element.38), channel_id=1, source_target_pairs={{0,4},{2,6},{4,0},{6,2},{8,12},{10,14},{12,8},{14,10},{16,20},{18,... | collective-permute-start | bytes 1572872 | tf_op jit(solution)/shard_map/ppermute | solution.py:450
  4.4 15.9 %collective-permute-start.3 = (bf16[256,1024]{1,0:T(8,128)(2,1)S(1)}, bf16[256,1024]{1,0:T(8,128)(2,1)S(1)}, u32[]{:S(2)}, u32[]{:S(2)}) collective-permute-start(bf16[256,1024]{1,0:T(8,128)(2,1)S(1)} %get-tuple-element.37.first_ref.refs_6_), channel_id=1, source_target_pairs={{4,12},{6,14},{8,0},{10,2},{12,20},{14,22},{16,8},{18,10},{20,28},... | collective-permute-start | bytes 1572872 | tf_op jit(solution)/shard_map/ppermute | solution.py:450
  5.7 0.8 %copy-start.9 = (bf16[256,1024]{1,0:T(8,128)(2,1)}, bf16[256,1024]{1,0:T(8,128)(2,1)S(1)}, u32[]{:S(2)}) copy-start(bf16[256,1024]{1,0:T(8,128)(2,1)S(1)} %collective-permute-done.1.beside_ref) | copy-start | bytes 1572868
  16.9 7.4 %copy-start.4 = (bf16[256,1024]{1,0:T(8,128)(2,1)}, bf16[256,1024]{1,0:T(8,128)(2,1)S(1)}, u32[]{:S(2)}) copy-start(bf16[256,1024]{1,0:T(8,128)(2,1)S(1)} %collective-permute-done.refs_0_) | copy-start | bytes 1572868
  20.3 4.1 %copy-start.5 = (bf16[256,1024]{1,0:T(8,128)(2,1)}, bf16[256,1024]{1,0:T(8,128)(2,1)S(1)}, u32[]{:S(2)}) copy-start(bf16[256,1024]{1,0:T(8,128)(2,1)S(1)} %collective-permute-done.3.refs_2_) | copy-start | bytes 1572868
  20.3 4.0 %collective-permute-start.4 = (bf16[256,1024]{1,0:T(8,128)(2,1)S(1)}, bf16[256,1024]{1,0:T(8,128)(2,1)S(1)}, u32[]{:S(2)}, u32[]{:S(2)}) collective-permute-start(bf16[256,1024]{1,0:T(8,128)(2,1)S(1)} %collective-permute-done.3.refs_2_), channel_id=1, source_target_pairs={{0,2},{2,0},{4,6},{6,4},{8,10},{10,8},{12,14},{14,12},{16,18},{18,... | collective-permute-start | bytes 1572872 | tf_op jit(solution)/shard_map/ppermute | solution.py:450
  20.3 4.0 %collective-permute-start.2 = (bf16[256,1024]{1,0:T(8,128)(2,1)S(1)}, bf16[256,1024]{1,0:T(8,128)(2,1)S(1)}, u32[]{:S(2)}, u32[]{:S(2)}) collective-permute-start(bf16[256,1024]{1,0:T(8,128)(2,1)S(1)} %collective-permute-done.refs_0_), channel_id=1, source_target_pairs={{0,2},{2,0},{4,6},{6,4},{8,10},{10,8},{12,14},{14,12},{16,18},{18,... | collective-permute-start | bytes 1572872 | tf_op jit(solution)/shard_map/ppermute | solution.py:450
  20.8 23.1 %collective-permute-start.5 = (bf16[256,1024]{1,0:T(8,128)(2,1)S(1)}, bf16[256,1024]{1,0:T(8,128)(2,1)S(1)}, u32[]{:S(2)}, u32[]{:S(2)}) collective-permute-start(bf16[256,1024]{1,0:T(8,128)(2,1)S(1)} %collective-permute-done.refs_0_), channel_id=1, source_target_pairs={{0,8},{2,10},{8,16},{10,18},{12,4},{14,6},{16,24},{18,26},{20,12},... | collective-permute-start | bytes 1572872 | tf_op jit(solution)/shard_map/ppermute | solution.py:450
  24.3 0.8 %copy-start.7 = (bf16[256,1024]{1,0:T(8,128)(2,1)}, bf16[256,1024]{1,0:T(8,128)(2,1)S(1)}, u32[]{:S(2)}) copy-start(bf16[256,1024]{1,0:T(8,128)(2,1)S(1)} %collective-permute-done.4.refs_3_) | copy-start | bytes 1572868
  24.3 0.9 %copy-start.8 = (bf16[256,1024]{1,0:T(8,128)(2,1)}, bf16[256,1024]{1,0:T(8,128)(2,1)S(1)}, u32[]{:S(2)}) copy-start(bf16[256,1024]{1,0:T(8,128)(2,1)S(1)} %collective-permute-done.2.refs_1_) | copy-start | bytes 1572868
  25.3 18.8 %copy-start.12 = (bf16[4,4]{1,0:T(4,128)(2,1)S(1)}, bf16[4,4]{1,0:T(4,128)(2,1)}, u32[]{:S(2)}) copy-start(bf16[4,4]{1,0:T(4,128)(2,1)} %param.15) | copy-start | bytes 100
  43.9 3.7 %copy-start.3 = (bf16[256,1024]{1,0:T(8,128)(2,1)}, bf16[256,1024]{1,0:T(8,128)(2,1)S(1)}, u32[]{:S(2)}) copy-start(bf16[256,1024]{1,0:T(8,128)(2,1)S(1)} %collective-permute-done.5.refs_0_) | copy-start | bytes 1572868
  43.9 3.7 %collective-permute-start.6 = (bf16[256,1024]{1,0:T(8,128)(2,1)S(1)}, bf16[256,1024]{1,0:T(8,128)(2,1)S(1)}, u32[]{:S(2)}, u32[]{:S(2)}) collective-permute-start(bf16[256,1024]{1,0:T(8,128)(2,1)S(1)} %collective-permute-done.5.refs_0_), channel_id=1, source_target_pairs={{0,2},{2,0},{4,6},{6,4},{8,10},{10,8},{12,14},{14,12},{16,18},{18,... | collective-permute-start | bytes 1572872 | tf_op jit(solution)/shard_map/ppermute | solution.py:450
  44.0 20.7 %collective-permute-start.7 = (bf16[256,1024]{1,0:T(8,128)(2,1)}, bf16[256,1024]{1,0:T(8,128)(2,1)S(1)}, u32[]{:S(2)}, u32[]{:S(2)}) collective-permute-start(bf16[256,1024]{1,0:T(8,128)(2,1)} %get-tuple-element.33), channel_id=1, source_target_pairs={{0,4},{2,6},{4,0},{6,2},{8,12},{10,14},{12,8},{14,10},{16,20},{18,... | collective-permute-start | bytes 1572872 | tf_op jit(solution)/shard_map/ppermute | solution.py:450
  44.7 21.2 %collective-permute-start.9 = (bf16[256,512]{1,0:T(8,128)(2,1)}, bf16[256,512]{1,0:T(8,128)(2,1)S(1)}, u32[]{:S(2)}, u32[]{:S(2)}) collective-permute-start(bf16[256,512]{1,0:T(8,128)(2,1)} %get-tuple-element.36), channel_id=1, source_target_pairs={{1,4},{3,6},{5,0},{7,2},{9,12},{11,14},{13,8},{15,10},{17,20},{19,... | collective-permute-start | bytes 786440 | tf_op jit(solution)/shard_map/ppermute | solution.py:492
  47.6 0.8 %copy-start.6 = (bf16[256,1024]{1,0:T(8,128)(2,1)}, bf16[256,1024]{1,0:T(8,128)(2,1)S(1)}, u32[]{:S(2)}) copy-start(bf16[256,1024]{1,0:T(8,128)(2,1)S(1)} %collective-permute-done.6.refs_1_) | copy-start | bytes 1572868
  48.4 16.3 %copy-start = (bf16[1024,512]{1,0:T(8,128)(2,1)S(1)}, bf16[1024,512]{1,0:T(8,128)(2,1)}, u32[]{:S(2)}) copy-start(bf16[1024,512]{1,0:T(8,128)(2,1)} %refs_11_.1) | copy-start | bytes 3145732
  64.1 8.4 %collective-permute-start.8 = (bf16[256,512]{1,0:T(8,128)(2,1)}, bf16[256,512]{1,0:T(8,128)(2,1)S(1)}, u32[]{:S(2)}, u32[]{:S(2)}) collective-permute-start(bf16[256,512]{1,0:T(8,128)(2,1)} %get-tuple-element.34.refs_2_), channel_id=1, source_target_pairs={{1,0},{0,1},{3,2},{2,3},{5,4},{4,5},{7,6},{6,7},{9,8},{8,9},{11,10... | collective-permute-start | bytes 786440 | tf_op jit(solution)/shard_map/ppermute | solution.py:503
  64.7 7.8 %copy-start.2 = (bf16[256,1024]{1,0:T(8,128)(2,1)}, bf16[256,1024]{1,0:T(8,128)(2,1)S(1)}, u32[]{:S(2)}) copy-start(bf16[256,1024]{1,0:T(8,128)(2,1)S(1)} %collective-permute-done.7.refs_1_) | copy-start | bytes 1572868
  65.9 6.6 %copy-start.10 = (bf16[256,512]{1,0:T(8,128)(2,1)}, bf16[256,512]{1,0:T(8,128)(2,1)S(1)}, u32[]{:S(2)}) copy-start(bf16[256,512]{1,0:T(8,128)(2,1)S(1)} %collective-permute-done.9.refs_5_) | copy-start | bytes 786436
  72.5 0.7 copy-start.11

commit v4 on v3

--- a/solution.py
+++ b/solution.py
@@ -19,7 +19,7 @@
     last = count // 4 - 1
     chip_swap = [(i, i ^ 2) for i in range(count)]
     core_swap = [(i, i ^ 1) for i in range(count)]
-    near, far = [], []
+    near, far, far_cross = [], [], []
     for i in range(count):
         quad, chip, core = i // 4, (i // 2) % 2, i % 2
         down = quad - 1 if quad > 0 else None
@@ -29,7 +29,9 @@
             near.append((i, place(near_quad, chip, core)))
         if far_quad is not None:
             far.append((i, place(far_quad, chip, core)))
-    return chip_swap, core_swap, near, far
+            if core != chip:
+                far_cross.append((i, place(far_quad, chip, chip)))
+    return chip_swap, core_swap, near, far, far_cross
 
 
 def project(first, beside, weight, scale):
@@ -83,7 +85,9 @@
     rows, width = raw[0].shape
     devices = lax.axis_size("tm")
     head_size = width // HEADS
-    pairs = width // LANES
+    chunk = 2 * LANES
+    chunks = width // chunk
+    pairs = chunk // LANES
     reach = WINDOW // rows
     steps = 2 * reach + 1
     slot_count = steps + 1
@@ -108,7 +112,7 @@
         wk_ref, wv_ref, wo_hbm, down_hbm = take(4)
         hidden_ref, branch_ref = take(2)
         keep_refs = take(2) if keep else None
-        key_scr, weight_scr, row_scr, query_scr = take(4)
+        key_scr, row_scr, query_scr = take(3)
         value_scrs, score_scrs, top_scrs = take(2), take(2), take(2)
         attended_scr, wo_scr, down_scr, copy_sems = take(4)
         index = pl.program_id(0)
@@ -135,7 +139,7 @@
                 copy.start()
             row_scr[...] = lax.broadcasted_iota(jnp.int32, (rows, LANES), 0)
 
-        def front(parity, value_scr, score_scr, top_scr):
+        def front(value_scr, score_scr, top_scr):
             units = []
             state = {}
 
@@ -145,8 +149,6 @@
                         slot = slot_of(ready_sides[number], which)
                         key_scr[slot] = ready_refs[2 * number][which]
                         value_scr[slot] = ready_refs[2 * number + 1][which]
-                weight_scr[:, :LANES] = wk_ref[...]
-                weight_scr[:, LANES:] = wv_ref[...]
 
             units.append(ready_blocks)
 
@@ -154,40 +156,44 @@
                 both = jnp.dot(raw_refs[0][...], wq_ref[...], preferred_element_type=jnp.float32)
                 query_scr[...] = (both * scale).astype(jnp.bfloat16)
 
-            if query_ref is None and parity == 0:
+            if query_ref is None:
                 units.append(project_queries)
 
-            def project_block(number, part):
+            def project_keys(number):
                 slot = slot_of(raw_sides[number // 2], number % 2)
-                where = slice(part * half_rows, (part + 1) * half_rows)
-                both = jnp.dot(
-                    raw_refs[number][where, :], weight_scr[...], preferred_element_type=jnp.float32
+                keys = jnp.dot(
+                    raw_refs[number][...], wk_ref[...], preferred_element_type=jnp.float32
                 ).astype(jnp.bfloat16)
-                keys, values = both[:, :LANES], both[:, LANES:].T
-                key_scr[slot, where, :] = keys
-                value_scr[slot, :, where] = values
+                key_scr[slot] = keys
                 if number < keep:
-                    keep_refs[0][number, where, :] = keys
-                    keep_refs[1][number, :, where] = values
-
-            for number in range(raw_count):
-                for part in range(2):
-                    units.append(functools.partial(project_block, number, part))
+                    keep_refs[0][number] = keys
+
+            def project_values(number):
+                slot = slot_of(raw_sides[number // 2], number % 2)
+                values = jnp.dot(
+                    raw_refs[number][...], wv_ref[...], preferred_element_type=jnp.float32
+                ).astype(jnp.bfloat16).T
+                value_scr[slot] = values
+                if number < keep:
+                    keep_refs[1][number] = values
+
+            for project in (project_keys, project_values):
+                for number in range(raw_count):
+                    units.append(functools.partial(project, number))
             early = len(units)
 
-            def bounds(half):
+            def bounds(pair, half):
                 column = lax.broadcasted_iota(jnp.int32, (1, cols), 1)
                 second = column >= half_rows
-                window = jnp.where(second, window_ref[2 * index + 1], window_ref[2 * index])
+                head = 2 * (pairs * index + pair)
+                window = jnp.where(second, window_ref[head + 1], window_ref[head])
                 lane = lax.broadcasted_iota(jnp.int32, (half_rows, LANES), 1)
                 local = jnp.where(second, column - half_rows, column) + half * half_rows
                 lowest = jnp.maximum(local - window, valid_first - query_first)
                 highest = jnp.minimum(local + window, patches - 1 - query_first)
                 where = slice(half * half_rows, (half + 1) * half_rows)
-                if query_ref is None:
-                    part = query_scr[where, parity * LANES : (parity + 1) * LANES]
-                else:
-                    part = query_ref[where, :]
+                source = query_scr if query_ref is None else query_ref
+                part = source[where, pair * LANES : (pair + 1) * LANES]
                 zero = jnp.zeros_like(part)
                 right = jnp.concatenate(
                     [
@@ -198,14 +204,14 @@
                 )
                 return right, lowest, highest
 
-            def score_block(half, step):
+            def score_block(pair, half, step):
                 if step == 0:
-                    state[half] = bounds(half)
-                right, lowest, highest = state[half]
+                    state["bounds"] = bounds(pair, half)
+                right, lowest, highest = state["bounds"]
                 start, stop = span(step, half)
                 first = (step - reach) * rows
                 scores = lax.dot_general(
-                    key_scr[core + step, start:stop, :],
+                    key_scr[core + step, start:stop, pair * LANES : (pair + 1) * LANES],
                     right,
                     (((1,), (1,)), ((), ())),
                     preferred_element_type=jnp.float32,
@@ -219,29 +225,31 @@
                     upper = key_row <= highest - first
                     allowed = upper if allowed is None else allowed & upper
                 scores = jnp.where(allowed, scores, MASKED)
-                score_scr[half, step, start:stop, :] = scores
+                score_scr[pair, half, step, start:stop, :] = scores
                 top = jnp.max(scores, axis=0, keepdims=True)
                 if step > 0:
                     top = jnp.maximum(state["top"], top)
                 state["top"] = top
                 if step == steps - 1:
-                    top_scr[half] = top
-
-            for half in range(2):
-                for step in range(steps):
-                    units.append(functools.partial(score_block, half, step))
+                    top_scr[pair, half] = top
+
+            for pair in range(pairs):
+                for half in range(2):
+                    for step in range(steps):
+                        units.append(functools.partial(score_block, pair, half, step))
             return units[:early], units[early:]
 
         def back(value_scr, score_scr, top_scr):
-            sums = [None, None]
-
-            def add_block(step, head):
+            sums = [None] * (2 * pairs)
+
+            def add_block(pair, step, head):
                 where = slice(head * half_rows, (head + 1) * half_rows)
                 parts = []
                 for half in range(2):
                     start, stop = span(step, half)
                     part = jnp.exp2(
-                        score_scr[half, step, start:stop, where] - top_scr[half][:, where]
+                        score_scr[pair, half, step, start:stop, where]
+                        - top_scr[pair, half][:, where]
                     )
                     part = [part.astype(jnp.bfloat16)]
                     if start > 0:
@@ -250,34 +258,39 @@
                         part = part + [jnp.zeros((rows - stop, half_rows), jnp.bfloat16)]
                     parts.append(jnp.concatenate(part, 0) if len(part) > 1 else part[0])
                 weights = jnp.concatenate(parts, 1)
+                first = pair * LANES + head * head_size
                 left = jnp.concatenate(
                     [
-                        value_scr[core + step, head * head_size : (head + 1) * head_size, :],
+                        value_scr[core + step, first : first + head_size, :],
                         jnp.ones((16, rows), jnp.bfloat16),
                     ],
                     0,
                 )
                 add = jnp.dot(left, weights, preferred_element_type=jnp.float32)
-                sums[head] = add if sums[head] is None else sums[head] + add
-
-            def write():
+                place = 2 * pair + head
+                sums[place] = add if sums[place] is None else sums[place] + add
+
+            def write(pair):
                 query_valid = (
                     lax.broadcasted_iota(jnp.int32, (1, rows), 1) >= valid_first - query_first
                 )
                 outs = []
                 for head in range(2):
-                    total = sums[head][head_size : head_size + 1]
+                    result = sums[2 * pair + head]
+                    total = result[head_size : head_size + 1]
                     factor = jnp.where(query_valid, 1.0 / total, 0.0)
-                    outs.append(sums[head][:head_size] * factor)
-                where = pl.ds(pl.multiple_of(jnp.maximum(index - 1, 0) * LANES, LANES), LANES)
+                    outs.append(result[:head_size] * factor)
+                first = jnp.maximum(index - 1, 0) * chunk + pair * LANES
+                where = pl.ds(pl.multiple_of(first, LANES), LANES)
                 attended_scr[:, where] = jnp.concatenate(outs, 0).T.astype(jnp.bfloat16)
 
-            units = [
-                functools.partial(add_block, step, head)
-                for head in range(2)
-                for step in range(steps)
-            ]
-            return units + [write]
+            units = []
+            for pair in range(pairs):
+                for head in range(2):
+                    for step in range(steps):
+                        units.append(functools.partial(add_block, pair, step, head))
+                units.append(functools.partial(write, pair))
+            return units
 
         def interleave(first, second):
             done = 0
@@ -291,15 +304,15 @@
         sets = [(value_scrs[n], score_scrs[n], top_scrs[n]) for n in range(2)]
         for parity in range(2):
 
-            @pl.when((index < pairs) & (index % 2 == parity))
+            @pl.when((index < chunks) & (index % 2 == parity))
             def _():
-                early, late = front(parity, *sets[parity])
+                early, late = front(*sets[parity])
                 interleave(early, back(*sets[1 - parity]))
                 interleave(late, [])
 
-        @pl.when(index == pairs)
+        @pl.when(index == chunks)
         def _():
-            for unit in back(*sets[(pairs - 1) % 2]):
+            for unit in back(*sets[(chunks - 1) % 2]):
                 unit()
             for copy in copies:
                 copy.wait()
@@ -310,12 +323,12 @@
                 hidden, down_scr[...], preferred_element_type=jnp.float32
             ).astype(jnp.bfloat16)
 
-    ahead = lambda g: jnp.minimum(g, pairs - 1)
-    block = pl.BlockSpec((rows, LANES), lambda g, *_: (0, ahead(g)))
-    key_spec = lambda count: pl.BlockSpec((count, rows, LANES), lambda g, *_: (0, 0, ahead(g)))
-    value_spec = lambda count: pl.BlockSpec((count, LANES, rows), lambda g, *_: (0, ahead(g), 0))
+    ahead = lambda g: jnp.minimum(g, chunks - 1)
+    block = pl.BlockSpec((rows, chunk), lambda g, *_: (0, ahead(g)))
+    key_spec = lambda count: pl.BlockSpec((count, rows, chunk), lambda g, *_: (0, 0, ahead(g)))
+    value_spec = lambda count: pl.BlockSpec((count, chunk, rows), lambda g, *_: (0, ahead(g), 0))
     weight_spec = lambda part: pl.BlockSpec(
-        (width, LANES), lambda g, *_: (0, part * pairs + ahead(g))
+        (width, chunk), lambda g, *_: (0, part * chunks + ahead(g))
     )
     in_specs = [pl.BlockSpec((rows, width), lambda g, *_: (0, 0)) for _ in raw]
     operands = list(raw)
@@ -327,9 +340,7 @@
         in_specs += [whole((rows, width)), block]
         operands += own
     else:
-        in_specs.append(
-            pl.BlockSpec((width, 2 * LANES), lambda g, *_: (0, ahead(g) // 2))
-        )
+        in_specs.append(weight_spec(0))
         operands.append(weight)
     in_specs += [weight_spec(1), weight_spec(2)] + [pl.BlockSpec(memory_space=pl.ANY)] * 2
     operands += [weight, weight, output_proj, mixer_down]
@@ -351,18 +362,17 @@
         out_shape=tuple(out_shape),
         grid_spec=pltpu.PrefetchScalarGridSpec(
             num_scalar_prefetch=3,
-            grid=(pairs + 1,),
+            grid=(chunks + 1,),
             in_specs=in_specs,
             out_specs=tuple(out_specs),
             scratch_shapes=[
-                pltpu.VMEM((slot_count, rows, LANES), jnp.bfloat16),
-                pltpu.VMEM((width, 2 * LANES), jnp.bfloat16),
+                pltpu.VMEM((slot_count, rows, chunk), jnp.bfloat16),
                 pltpu.VMEM((rows, LANES), jnp.int32),
-                pltpu.VMEM((rows, 2 * LANES), jnp.bfloat16),
+                pltpu.VMEM((rows, chunk), jnp.bfloat16),
             ]
-            + twice((slot_count, LANES, rows), jnp.bfloat16)
-            + twice((2, steps, rows, cols), jnp.float32)
-            + twice((2, 1, cols), jnp.float32)
+            + twice((slot_count, chunk, rows), jnp.bfloat16)
+            + twice((pairs, 2, steps, rows, cols), jnp.float32)
+            + twice((pairs, 2, 1, cols), jnp.float32)
             + [
                 pltpu.VMEM((rows, width), jnp.bfloat16),
                 pltpu.VMEM(output_proj.shape, jnp.bfloat16),
@@ -381,7 +391,6 @@
 
 def mix(place, own_group, series_mix, weight, hidden, branches):
     rows, width = hidden[0].shape
-    inner = weight.shape[0]
     groups = len(branches[0])
 
     def body(place_ref, group_ref, mix_ref, weight_ref, *refs):
@@ -390,45 +399,31 @@
         out_ref = refs[-1]
         own = group_ref[0]
         chip = (place_ref[0] // 2) % 2
+        series = [chip, 1 - chip]
         for which in range(2):
-
-            @pl.when(pl.program_id(0) == which)
-            def _():
-                series = [chip, 1 - chip]
-                row = 2 * own + series[which]
-                total = None
-                for number, branch_ref in enumerate(branch_refs):
-                    kind, shift = number // groups, number % groups
-                    group = (own + shift) % groups
-                    term = mix_ref[row, 2 * group + series[kind]] * branch_ref[...].astype(
-                        jnp.float32
-                    )
-                    total = term if total is None else total + term
-                update = jnp.dot(
-                    total.astype(jnp.bfloat16), weight_ref[...], preferred_element_type=jnp.float32
-                )
-                out_ref[0] = (hidden_refs[which][...].astype(jnp.float32) + update).astype(
-                    out_ref.dtype
-                )
-
-    def out_index(which, place_ref, *_):
-        chip = (place_ref[0] // 2) % 2
-        return chip + which - 2 * chip * which, 0, 0
-
-    whole = lambda shape: pl.BlockSpec(shape, lambda which, *_: (0, 0))
+            row = 2 * own + series[which]
+            total = None
+            for number, branch_ref in enumerate(branch_refs):
+                kind, shift = number // groups, number % groups
+                group = (own + shift) % groups
+                term = mix_ref[row, 2 * group + series[kind]] * branch_ref[...].astype(jnp.float32)
+                total = term if total is None else total + term
+            update = jnp.dot(
+                total.astype(jnp.bfloat16), weight_ref[...], preferred_element_type=jnp.float32
+            )
+            out_ref[series[which]] = (
+                hidden_refs[which][...].astype(jnp.float32) + update
+            ).astype(out_ref.dtype)
+
+    small = pl.BlockSpec(memory_space=pltpu.SMEM)
+    large = pl.BlockSpec(memory_space=pltpu.VMEM)
     return pl.pallas_call(
         body,
         out_shape=jax.ShapeDtypeStruct((2, rows, width), jnp.bfloat16),
-        grid_spec=pltpu.PrefetchScalarGridSpec(
-            num_scalar_prefetch=3,
-            grid=(2,),
-            in_specs=[whole((inner, width))]
-            + [whole((rows, width))] * 2
-            + [whole((rows, inner))] * (2 * groups),
-            out_specs=pl.BlockSpec((1, rows, width), out_index),
-        ),
+        in_specs=[small] * 3 + [large] * (3 + 2 * groups),
+        out_specs=large,
         cost_estimate=pl.CostEstimate(
-            flops=4 * rows * inner * width, bytes_accessed=2 * inner * width, transcendentals=0
+            flops=4 * rows * weight.size, bytes_accessed=2 * weight.size, transcendentals=0
         ),
         name="mix",
     )(place, own_group, series_mix, weight, *hidden, *branches[0], *branches[1])
@@ -441,10 +436,9 @@
     devices = lax.axis_size("tm")
     groups = lax.axis_size("series")
     assert local_series == 2 and devices % 4 == 0 and WINDOW == 2 * rows
-    patches = rows * devices
     position = lax.axis_index("tm")
-    quad, chip, core = position // 4, (position // 2) % 2, position % 2
-    chip_swap, core_swap, near_route, far_route = routes(devices)
+    chip = (position // 2) % 2
+    chip_swap, core_swap, near_route, far_route, far_cross = routes(devices)
 
     def move(block, route):
         return lax.ppermute(block, "tm", route)
@@ -465,18 +459,18 @@
 
     home_queries, *home_ready = project(mine, mine_beside, input_proj, scale)
     away, home_queries = lax.optimization_barrier((away, home_queries))
+    away_beside = move(away, core_swap)
+    near, away_beside = lax.optimization_barrier((near, away_beside))
+    near_beside = move(near, core_swap)
     far = move(away, far_route)
-    away_beside = move(away, core_swap)
-    near, home_queries = lax.optimization_barrier((near, home_queries))
-    near_beside = move(near, core_swap)
+    far_beside = move(away, far_cross)
     away_hidden, away_branch, *away_ready = attention(
         False,
         [(0, [away, away_beside]), (1, [near, near_beside])],
         [(-1, home_ready)],
         keep=2,
     )
-    away_hidden, far = lax.optimization_barrier((away_hidden, far))
-    far_beside = move(far, core_swap)
+    away_hidden, far, far_beside = lax.optimization_barrier((away_hidden, far, far_beside))
 
     def down(hidden):
         return jnp.dot(hidden, mixer_down, preferred_element_type=jnp.float32).astype(jnp.bfloat16)

time: 78.1 us -> 76.9 us (0.985); the launches traced: 77.7 us -> 75.6 us
  Pallas kernels: 45.8 us -> 40.9 us
  waiting for transfers between devices: 13.3 us -> 16.9 us
  local copies, waits for them, and re-layouts: 4.53 us -> 3.71 us
    ppermute x1, waiting for transfers between devices: 0.01 us -> 7.05 us  [on_device(): other_branches.append(lax.ppermute(away_branch, ('tm', 'series'), route))]
    pallas_call x2, Pallas kernels: 34.3 us -> 30.2 us  [attend(): pl.pallas_call(body, out_shape=tuple(out_shape), grid_spec=pltpu.Prefetch...]
    ppermute x1, waiting for transfers between devices: 6.61 us -> 3.09 us  [on_device(): mine_branches.append(lax.ppermute(mine_branch, 'series', route))]
    ppermute x1, starting transfers between devices: 2.94 us -> 1.71 us  [on_device(): other_branches.append(lax.ppermute(away_branch, ('tm', 'series'), route))]
    ppermute x1, starting transfers between devices: 0.6 us -> 1.57 us  [on_device(): mine_branches.append(lax.ppermute(mine_branch, 'series', route))]
    unnamed x26 -> x28, local copies, waits for them, and re-layouts: 3.27 us -> 2.44 us
    pallas_call x1, Pallas kernels: 4.5 us -> 3.69 us  [mix(): pl.pallas_call(body, out_shape=jax.ShapeDtypeStruct((2, rows, width), jnp...]
  transfers between devices with their start and end apart: 10 -> 10, of which waited for: 3 -> 4; matrix products, arithmetic and copies ran while one was open for 2% -> 2% of each run, Pallas kernels for 53% -> 49%
where the time goes in v4:
time: 76.9 us; the launch traced here: 75.6 us
  Pallas kernels  40.9 us (53%)
  waiting for transfers between devices  16.9 us (22%)
  starting transfers between devices  12 us (16%)
  local copies, waits for them, and re-layouts  3.71 us (5%)
  matrix products  1.15 us (1%)
    pallas_call x2, Pallas kernels, attend(): pl.pallas_call(body, out_shape=tuple(out_shape), grid_spec=pltpu.Prefetch...  30.2 us
    ppermute x8, starting transfers between devices, move(): return lax.ppermute(block, 'tm', route)  8.77 us
    ppermute x1, waiting for transfers between devices, on_device(): other_branches.append(lax.ppermute(away_branch, ('tm', 'series'), route))  7.05 us
    pallas_call x1, Pallas kernels, project(): pl.pallas_call(body, out_shape=(jax.ShapeDtypeStruct((rows, width), jnp.b...  7.02 us
    ppermute x8, waiting for transfers between devices, move(): return lax.ppermute(block, 'tm', route)  6.74 us
    pallas_call x1, Pallas kernels, mix(): pl.pallas_call(body, out_shape=jax.ShapeDtypeStruct((2, rows, width), jnp...  3.69 us
    ppermute x1, waiting for transfers between devices, on_device(): mine_branches.append(lax.ppermute(mine_branch, 'series', route))  3.09 us
    unnamed x28, local copies, waits for them, and re-layouts  2.44 us
  transfers between devices with their start and end apart: 10, of which 4 were waited for; matrix products, arithmetic and copies ran while one was open for 2% of the time, Pallas kernels for 49%

profile of v4, /device:TPU:0, one launch (start us, length us, event | category | flops | bytes accessed | tf_op | source)
XLA Modules:
  0.0 75.6 jit_solution(2667997321014611991)
XLA Ops:
  0.0 1.3 %dynamic-slice_bitcast_fusion = (bf16[256,1024]{1,0:T(8,128)(2,1)S(1)}, bf16[256,1024]{1,0:T(8,128)(2,1)S(1)}) fusion(bf16[2,256,1024]{2,1,0:T(8,128)(2,1)} %param.8, s32[]{:T(128)S(6)} %select_n.21, s32[]{:T(128)S(6)} %select_n.20), kind=kLoop, calls=%fused_computation.1 | loop fusion | bytes 2097160 | tf_op jit(solution)/shard_map/jit(dynamic_index_in_dim)/squeeze | solution.py:447
  1.3 0.6 collective-permute-start.1
  1.8 2.6 %collective-permute-start = (bf16[256,1024]{1,0:T(8,128)(2,1)S(1)}, bf16[256,1024]{1,0:T(8,128)(2,1)S(1)}, u32[]{:S(2)}, u32[]{:S(2)}) collective-permute-start(bf16[256,1024]{1,0:T(8,128)(2,1)S(1)} %get-tuple-element.40), channel_id=1, source_target_pairs={{0,4},{2,6},{4,0},{6,2},{8,12},{10,14},{12,8},{14,10},{16,20},{18,... | collective-permute-start | bytes 1572872 | tf_op jit(solution)/shard_map/ppermute | solution.py:444
  4.4 1.3 %collective-permute-start.2 = (bf16[256,1024]{1,0:T(8,128)(2,1)S(1)}, bf16[256,1024]{1,0:T(8,128)(2,1)S(1)}, u32[]{:S(2)}, u32[]{:S(2)}) collective-permute-start(bf16[256,1024]{1,0:T(8,128)(2,1)S(1)} %get-tuple-element.39.first_ref.refs_6_), channel_id=1, source_target_pairs={{4,12},{6,14},{8,0},{10,2},{12,20},{14,22},{16,8},{18,10},{20,28},... | collective-permute-start | bytes 1572872 | tf_op jit(solution)/shard_map/ppermute | solution.py:444
  5.7 0.0 collective-permute-done.1.beside_ref
  5.7 0.8 %copy-done.9 = bf16[256,1024]{1,0:T(8,128)(2,1)} copy-done((bf16[256,1024]{1,0:T(8,128)(2,1)}, bf16[256,1024]{1,0:T(8,128)(2,1)S(1)}, u32[]{:S(2)}) %copy-start.9) | copy-done | bytes 524312
  6.5 7.0 %project.1 = (bf16[256,1024]{1,0:T(8,128)(2,1)}, bf16[2,256,1024]{2,1,0:T(8,128)(2,1)}, bf16[2,1024,256]{2,1,0:T(8,128)(2,1)}) custom-call(bf16[256,1024]{1,0:T(8,128)(2,1)} %copy-done.1, bf16[256,1024]{1,0:T(8,128)(2,1)} %copy-done.9, bf16[1024,3072]{1,0:T(8,128)(2,1)} %refs_9_.3, bf16[1024,3072]{1,0:T(8,128)(2,1)} %refs_9_.3, bf16[1024,3072]{1,0:T(8,128)(2,1)} %refs_9_.3), custom_call_target="tpu_custom_call" | custom-call | flops 2684354560 | bytes 6291456 | tf_op jit(solution)/shard_map/project/pallas_call | solution.py:56
  13.6 3.4 %collective-permute-done.refs_0_ = bf16[256,1024]{1,0:T(8,128)(2,1)S(1)} collective-permute-done((bf16[256,1024]{1,0:T(8,128)(2,1)S(1)}, bf16[256,1024]{1,0:T(8,128)(2,1)S(1)}, u32[]{:S(2)}, u32[]{:S(2)}) %collective-permute-start) | collective-permute-done | bytes 524320 | tf_op jit(solution)/shard_map/ppermute | solution.py:444
  16.9 0.0 collective-permute-start.3
  16.9 3.3 %collective-permute-done.2.refs_2_ = bf16[256,1024]{1,0:T(8,128)(2,1)S(1)} collective-permute-done((bf16[256,1024]{1,0:T(8,128)(2,1)S(1)}, bf16[256,1024]{1,0:T(8,128)(2,1)S(1)}, u32[]{:S(2)}, u32[]{:S(2)}) %collective-permute-start.2) | collective-permute-done | bytes 524320 | tf_op jit(solution)/shard_map/ppermute | solution.py:444
  20.3 0.0 collective-permute-done.3.refs_1_
  20.3 0.1 collective-permute-start.4
  20.4 3.5 %collective-permute-start.5 = (bf16[256,1024]{1,0:T(8,128)(2,1)S(1)}, bf16[256,1024]{1,0:T(8,128)(2,1)S(1)}, u32[]{:S(2)}, u32[]{:S(2)}) collective-permute-start(bf16[256,1024]{1,0:T(8,128)(2,1)S(1)} %collective-permute-done.refs_0_), channel_id=1, source_target_pairs={{0,8},{2,10},{8,16},{10,18},{12,4},{14,6},{16,24},{18,26},{20,12},... | collective-permute-start | bytes 1572872 | tf_op jit(solution)/shard_map/ppermute | solution.py:444
  23.9 0.7 collective-permute-start.6
  24.6 0.0 collective-permute-done.4.refs_3_
  24.6 0.8 %copy-done.8 = bf16[256,1024]{1,0:T(8,128)(2,1)} copy-done((bf16[256,1024]{1,0:T(8,128)(2,1)}, bf16[256,1024]{1,0:T(8,128)(2,1)S(1)}, u32[]{:S(2)}) %copy-start.8) | copy-done | bytes 524312
  25.4 16.5 %attend.2 = (bf16[256,1024]{1,0:T(8,128)(2,1)}, bf16[256,512]{1,0:T(8,128)(2,1)}, bf16[2,256,1024]{2,1,0:T(8,128)(2,1)}, bf16[2,1024,256]{2,1,0:T(8,128)(2,1)}) custom-call(s32[1]{0:T(128)} %bitcast.place_ref, s32[16]{0:T(128)} %window_ref.3, s32[2]{0:T(128)} %length_ref.3, bf16[256,1024]{1,0:T(8,128)(2,1)} %copy-done.3, bf16[256,1024]{1,0:T(8,128)(2,1)} %copy-done.7, ...), custom_call_target="tpu_custom_call" | custom-call | flops 6979321856 | bytes 9437184 | tf_op jit(solution)/shard_map/attend/pallas_call | solution.py:360
  42.0 0.0 collective-permute-done.5.refs_0_
  42.0 0.0 collective-permute-done.6.refs_1_
  42.0 0.1 collective-permute-start.7
  42.1 0.7 convert_element_type.6.mix_ref
  42.8 0.2 copy-done.6
  42.9 13.7 %attend.3 = (bf16[256,1024]{1,0:T(8,128)(2,1)}, bf16[256,512]{1,0:T(8,128)(2,1)}) custom-call(s32[1]{0:T(128)} %bitcast.place_ref, s32[16]{0:T(128)} %window_ref.3, s32[2]{0:T(128)} %length_ref.3, bf16[256,1024]{1,0:T(8,128)(2,1)} %copy-done.5, bf16[256,1024]{1,0:T(8,128)(2,1)} %copy-done.6, bf16[2,256,1024]{2,1,0:T(8,128)(2,1)} %get-tuple-element.26.refs_4_.refs_2_, ...), custom_call_target="tpu_custom_call" | custom-call | flops 4831838208 | bytes 9437184 | tf_op jit(solution)/shard_map/attend/pallas_call | solution.py:360
  56.6 1.6 %collective-permute-start.8 = (bf16[256,512]{1,0:T(8,128)(2,1)}, bf16[256,512]{1,0:T(8,128)(2,1)S(1)}, u32[]{:S(2)}, u32[]{:S(2)}) collective-permute-start(bf16[256,512]{1,0:T(8,128)(2,1)} %get-tuple-element.36.refs_2_), channel_id=1, source_target_pairs={{1,0},{0,1},{3,2},{2,3},{5,4},{4,5},{7,6},{6,7},{9,8},{8,9},{11,10... | collective-permute-start | bytes 786440 | tf_op jit(solution)/shard_map/ppermute | solution.py:497
  58.2 0.0 copy-done.13
  58.2 1.7 %collective-permute-start.9 = (bf16[256,512]{1,0:T(8,128)(2,1)S(1)}, bf16[256,512]{1,0:T(8,128)(2,1)S(1)}, u32[]{:S(2)}, u32[]{:S(2)}) collective-permute-start(bf16[256,512]{1,0:T(8,128)(2,1)S(1)} %copy-done.13), channel_id=1, source_target_pairs={{1,4},{3,6},{5,0},{7,2},{9,12},{11,14},{13,8},{15,10},{17,20},{19,... | collective-permute-start | bytes 786440 | tf_op jit(solution)/shard_map/ppermute | solution.py:486
  59.9 0.0 collective-permute-done.7.refs_1_
  59.9 1.1 %convolution_convert_fusion.refs_4_ = bf16[256,512]{1,0:T(8,128)(2,1)} fusion(bf16[256,1024]{1,0:T(8,128)(2,1)S(1)} %collective-permute-done.7.refs_1_, bf16[1024,512]{1,0:T(8,128)(2,1)S(1)} %copy-done), kind=kOutput, calls=%fused_computation | convolution fusion | flops 268566528 | bytes 1835008 | tf_op jit(solution)/shard_map/dot_general | solution.py:476
  61.1 3.1 %collective-permute-done.8.refs_3_ = bf16[256,512]{1,0:T(8,128)(2,1)S(1)} collective-permute-done((bf16[256,512]{1,0:T(8,128)(2,1)}, bf16[256,512]{1,0:T(8,128)(2,1)S(1)}, u32[]{:S(2)}, u32[]{:S(2)}) %collective-permute-start.8) | collective-permute-done | bytes 262176 | tf_op jit(solution)/shard_map/ppermute | solution.py:497
  64.2 7.1 %collective-permute-done.9.refs_5_ = bf16[256,512]{1,0:T(8,128)(2,1)S(1)} collective-permute-done((bf16[256,512]{1,0:T(8,128)(2,1)S(1)}, bf16[256,512]{1,0:T(8,128)(2,1)S(1)}, u32[]{:S(2)}, u32[]{:S(2)}) %collective-permute-start.9) | collective-permute-done | bytes 262176 | tf_op jit(solution)/shard_map/ppermute | solution.py:486
  71.2 0.7 copy-done.11
  71.9 3.7 %mix.1 = bf16[2,256,1024]{2,1,0:T(8,128)(2,1)} custom-call(s32[1]{0:T(128)} %bitcast.place_ref, s32[1]{0:T(128)} %bitcast.1.group_ref, f32[4,4]{1,0:T(4,128)} %convert_element_type.6.mix_ref, bf16[512,1024]{1,0:T(8,128)(2,1)} %weight_ref.1, bf16[256,1024]{1,0:T(8,128)(2,1)} %get-tuple-element.34.refs_0_, bf16[256,1024]{1,0:T(8,128)(2,1)} %copy-done.2, ...), custom_call_target="tpu_custom_call" | custom-call | flops 536870912 | bytes 1048576 | tf_op jit(solution)/shard_map/mix/pallas_call | solution.py:420
  (23 shorter events, 0.0 us)
Async XLA Ops:
  1.3 4.5 %copy-start.1 = (bf16[256,1024]{1,0:T(8,128)(2,1)}, bf16[256,1024]{1,0:T(8,128)(2,1)S(1)}, u32[]{:S(2)}) copy-start(bf16[256,1024]{1,0:T(8,128)(2,1)S(1)} %get-tuple-element.39.first_ref.refs_6_) | copy-start | bytes 1572868
  1.3 4.4 %collective-permute-start.1 = (bf16[256,1024]{1,0:T(8,128)(2,1)S(1)}, bf16[256,1024]{1,0:T(8,128)(2,1)S(1)}, u32[]{:S(2)}, u32[]{:S(2)}) collective-permute-start(bf16[256,1024]{1,0:T(8,128)(2,1)S(1)} %get-tuple-element.39.first_ref.refs_6_), channel_id=1, source_target_pairs={{0,2},{2,0},{4,6},{6,4},{8,10},{10,8},{12,14},{14,12},{16,18},{18,... | collective-permute-start | bytes 1572872 | tf_op jit(solution)/shard_map/ppermute | solution.py:444
  1.8 15.1 %collective-permute-start = (bf16[256,1024]{1,0:T(8,128)(2,1)S(1)}, bf16[256,1024]{1,0:T(8,128)(2,1)S(1)}, u32[]{:S(2)}, u32[]{:S(2)}) collective-permute-start(bf16[256,1024]{1,0:T(8,128)(2,1)S(1)} %get-tuple-element.40), channel_id=1, source_target_pairs={{0,4},{2,6},{4,0},{6,2},{8,12},{10,14},{12,8},{14,10},{16,20},{18,... | collective-permute-start | bytes 1572872 | tf_op jit(solution)/shard_map/ppermute | solution.py:444
  4.4 15.9 %collective-permute-start.2 = (bf16[256,1024]{1,0:T(8,128)(2,1)S(1)}, bf16[256,1024]{1,0:T(8,128)(2,1)S(1)}, u32[]{:S(2)}, u32[]{:S(2)}) collective-permute-start(bf16[256,1024]{1,0:T(8,128)(2,1)S(1)} %get-tuple-element.39.first_ref.refs_6_), channel_id=1, source_target_pairs={{4,12},{6,14},{8,0},{10,2},{12,20},{14,22},{16,8},{18,10},{20,28},... | collective-permute-start | bytes 1572872 | tf_op jit(solution)/shard_map/ppermute | solution.py:444
  5.7 0.8 %copy-start.9 = (bf16[256,1024]{1,0:T(8,128)(2,1)}, bf16[256,1024]{1,0:T(8,128)(2,1)S(1)}, u32[]{:S(2)}) copy-start(bf16[256,1024]{1,0:T(8,128)(2,1)S(1)} %collective-permute-done.1.beside_ref) | copy-start | bytes 1572868
  16.9 7.7 %copy-start.3 = (bf16[256,1024]{1,0:T(8,128)(2,1)}, bf16[256,1024]{1,0:T(8,128)(2,1)S(1)}, u32[]{:S(2)}) copy-start(bf16[256,1024]{1,0:T(8,128)(2,1)S(1)} %collective-permute-done.refs_0_) | copy-start | bytes 1572868
  16.9 3.3 %collective-permute-start.3 = (bf16[256,1024]{1,0:T(8,128)(2,1)S(1)}, bf16[256,1024]{1,0:T(8,128)(2,1)S(1)}, u32[]{:S(2)}, u32[]{:S(2)}) collective-permute-start(bf16[256,1024]{1,0:T(8,128)(2,1)S(1)} %collective-permute-done.refs_0_), channel_id=1, source_target_pairs={{0,2},{2,0},{4,6},{6,4},{8,10},{10,8},{12,14},{14,12},{16,18},{18,... | collective-permute-start | bytes 1572872 | tf_op jit(solution)/shard_map/ppermute | solution.py:444
  20.3 4.3 %copy-start.4 = (bf16[256,1024]{1,0:T(8,128)(2,1)}, bf16[256,1024]{1,0:T(8,128)(2,1)S(1)}, u32[]{:S(2)}) copy-start(bf16[256,1024]{1,0:T(8,128)(2,1)S(1)} %collective-permute-done.2.refs_2_) | copy-start | bytes 1572868
  20.3 4.3 %copy-start.7 = (bf16[256,1024]{1,0:T(8,128)(2,1)}, bf16[256,1024]{1,0:T(8,128)(2,1)S(1)}, u32[]{:S(2)}) copy-start(bf16[256,1024]{1,0:T(8,128)(2,1)S(1)} %collective-permute-done.3.refs_1_) | copy-start | bytes 1572868
  20.3 4.3 %collective-permute-start.4 = (bf16[256,1024]{1,0:T(8,128)(2,1)S(1)}, bf16[256,1024]{1,0:T(8,128)(2,1)S(1)}, u32[]{:S(2)}, u32[]{:S(2)}) collective-permute-start(bf16[256,1024]{1,0:T(8,128)(2,1)S(1)} %collective-permute-done.2.refs_2_), channel_id=1, source_target_pairs={{0,2},{2,0},{4,6},{6,4},{8,10},{10,8},{12,14},{14,12},{16,18},{18,... | collective-permute-start | bytes 1572872 | tf_op jit(solution)/shard_map/ppermute | solution.py:444
  20.4 21.6 %collective-permute-start.5 = (bf16[256,1024]{1,0:T(8,128)(2,1)S(1)}, bf16[256,1024]{1,0:T(8,128)(2,1)S(1)}, u32[]{:S(2)}, u32[]{:S(2)}) collective-permute-start(bf16[256,1024]{1,0:T(8,128)(2,1)S(1)} %collective-permute-done.refs_0_), channel_id=1, source_target_pairs={{0,8},{2,10},{8,16},{10,18},{12,4},{14,6},{16,24},{18,26},{20,12},... | collective-permute-start | bytes 1572872 | tf_op jit(solution)/shard_map/ppermute | solution.py:444
  23.9 18.1 %collective-permute-start.6 = (bf16[256,1024]{1,0:T(8,128)(2,1)S(1)}, bf16[256,1024]{1,0:T(8,128)(2,1)S(1)}, u32[]{:S(2)}, u32[]{:S(2)}) collective-permute-start(bf16[256,1024]{1,0:T(8,128)(2,1)S(1)} %collective-permute-done.refs_0_), channel_id=1, source_target_pairs={{2,8},{10,16},{12,6},{18,24},{20,14},{28,22},{3,9},{11,17},{13,7},... | collective-permute-start | bytes 1572872 | tf_op jit(solution)/shard_map/ppermute | solution.py:444
  24.6 0.8 %copy-start.8 = (bf16[256,1024]{1,0:T(8,128)(2,1)}, bf16[256,1024]{1,0:T(8,128)(2,1)S(1)}, u32[]{:S(2)}) copy-start(bf16[256,1024]{1,0:T(8,128)(2,1)S(1)} %collective-permute-done.4.refs_3_) | copy-start | bytes 1572868
  25.4 16.7 %copy-start.12 = (bf16[4,4]{1,0:T(4,128)(2,1)S(1)}, bf16[4,4]{1,0:T(4,128)(2,1)}, u32[]{:S(2)}) copy-start(bf16[4,4]{1,0:T(4,128)(2,1)} %param.15) | copy-start | bytes 100
  42.0 0.8 %copy-start.5 = (bf16[256,1024]{1,0:T(8,128)(2,1)}, bf16[256,1024]{1,0:T(8,128)(2,1)S(1)}, u32[]{:S(2)}) copy-start(bf16[256,1024]{1,0:T(8,128)(2,1)S(1)} %collective-permute-done.5.refs_0_) | copy-start | bytes 1572868
  42.0 1.0 %copy-start.6 = (bf16[256,1024]{1,0:T(8,128)(2,1)}, bf16[256,1024]{1,0:T(8,128)(2,1)S(1)}, u32[]{:S(2)}) copy-start(bf16[256,1024]{1,0:T(8,128)(2,1)S(1)} %collective-permute-done.6.refs_1_) | copy-start | bytes 1572868
  42.0 17.9 %collective-permute-start.7 = (bf16[256,1024]{1,0:T(8,128)(2,1)}, bf16[256,1024]{1,0:T(8,128)(2,1)S(1)}, u32[]{:S(2)}, u32[]{:S(2)}) collective-permute-start(bf16[256,1024]{1,0:T(8,128)(2,1)} %get-tuple-element.35), channel_id=1, source_target_pairs={{0,4},{2,6},{4,0},{6,2},{8,12},{10,14},{12,8},{14,10},{16,20},{18,... | collective-permute-start | bytes 1572872 | tf_op jit(solution)/shard_map/ppermute | solution.py:444
  42.9 15.3 %copy-start.13 = (bf16[256,512]{1,0:T(8,128)(2,1)S(1)}, bf16[256,512]{1,0:T(8,128)(2,1)}, u32[]{:S(2)}) copy-start(bf16[256,512]{1,0:T(8,128)(2,1)} %get-tuple-element.38) | copy-start | bytes 786436
  42.9 17.0 %copy-start = (bf16[1024,512]{1,0:T(8,128)(2,1)S(1)}, bf16[1024,512]{1,0:T(8,128)(2,1)}, u32[]{:S(2)}) copy-start(bf16[1024,512]{1,0:T(8,128)(2,1)} %refs_11_.1) | copy-start | bytes 3145732
  56.6 7.5 %collective-permute-start.8 = (bf16[256,512]{1,0:T(8,128)(2,1)}, bf16[256,512]{1,0:T(8,128)(2,1)S(1)}, u32[]{:S(2)}, u32[]{:S(2)}) collective-permute-start(bf16[256,512]{1,0:T(8,128)(2,1)} %get-tuple-element.36.refs_2_), channel_id=1, source_target_pairs={{1,0},{0,1},{3,2},{2,3},{5,4},{4,5},{7,6},{6,7},{9,8},{8,9},{11,10... | collective-permute-start | bytes 786440 | tf_op jit(solution)/shard_map/ppermute | solution.py:497
  58.2 13.0 %collective-permute-start.9 = (bf16[256,512]{1,0:T(8,128)(2,1)S(1)}, bf16[256,512]{1,0:T(8,128)(2,1)S(1)}, u32[]{:S(2)}, u32[]{:S(2)}) collective-permute-start(bf16[256,512]{1,0:T(8,128)(2,1)S(1)} %copy-done.13), channel_id=1, source_target_pairs={{1,4},{3,6},{5,0},{7,2},{9,12},{11,14},{13,8},{15,10},{17,20},{19,... | collective-permute-start | bytes 786440 | tf_op jit(solution)/shard_map/ppermute | solution.py:486
  59.9 11.3 %copy-start.2 = (bf16[256,1024]{1,0:T(8,128)(2,1)}, bf16[256,1024]{1,0:T(8,128)(2,1)S(1)}, u32[]{:S(2)}) copy-start(bf16[256,1024]{1,0:T(8,128)(2,1)S(1)} %collective-permute-done.7.refs_1_) | copy-start | bytes 1572868
  64.2 7.1 %copy-start.10 = (bf16[256,512]{1,0:T(8,128)(2,1)}, bf16[256,512]{1,0:T(8,128)(2,1)S(1)}, u32[]{:S(2)}) copy-start(bf16[256,512]{1,0:T(8,128)(2,1)S(1)} %collective-permute-done.8.refs_3_) | copy-start | bytes 786436
  71.2 0.7 copy-start.11
